TPU v7x, 8 devices: a whole 2x2x1 slice. The times are simulated.
8 devices in a mesh: dp: 2 (over z, y), tp: 4 (over x, core).
Axes of the slice: x: 2, y: 2, z: 1, core: 2. Of those that a mesh axis runs over, the one named last changes fastest.
Arguments:
- tokens: int32 [2, 2048], P('dp'), parts along dimension 0
- doc_ids: int32 [2, 2048], P('dp'), parts along dimension 0
- embedding: bfloat16 [32000, 2048], P('tp')
- attn_norm: bfloat16 [2048], replicated
- w_q: bfloat16 [2048, 32, 64], P(None, 'tp')
- w_k: bfloat16 [2048, 4, 64], P(None, 'tp')
- w_v: bfloat16 [2048, 4, 64], P(None, 'tp')
- w_o: bfloat16 [32, 64, 2048], P('tp')
- mlp_norm: bfloat16 [2048], replicated
- w_gate: bfloat16 [2048, 5632], P(None, 'tp')
- w_up: bfloat16 [2048, 5632], P(None, 'tp')
- w_down: bfloat16 [5632, 2048], P('tp')
- d_out: bfloat16 [2, 2048, 2048], P('dp', 'tp'), parts along dimension 0
Outputs:
- output 1: bfloat16 [2, 2048, 2048], P('dp', 'tp'), parts along dimension 0
- output 2: float32 [64000, 2048], P(('dp', 'tp')), parts along dimension 0
- output 3: float32 [4096], P('dp'), parts along dimension 0
- output 4: float32 [4096, 32, 64], P('dp', 'tp'), parts along dimension 0
- output 5: float32 [4096, 4, 64], P('dp', 'tp'), parts along dimension 0
- output 6: float32 [4096, 4, 64], P('dp', 'tp'), parts along dimension 0
- output 7: float32 [64, 64, 2048], P(('dp', 'tp')), parts along dimension 0
- output 8: float32 [4096], P('dp'), parts along dimension 0
- output 9: float32 [4096, 5632], P('dp', 'tp'), parts along dimension 0
- output 10: float32 [4096, 5632], P('dp', 'tp'), parts along dimension 0
- output 11: float32 [11264, 2048], P(('dp', 'tp')), parts along dimension 0
There are 2 independent parts. A program takes and returns all parts, laid end to end along the dimension named above; an argument that names none is the same for every part.
All inputs are finite; a program needn't handle non-finite values.
Results may differ from a plain program's by a relative error of at most 0.02.
Values are sent between devices in bfloat16 or wider.
A program may use at most 1 GiB of HBM per device.

v0:
```python
import math
import jax
import jax.numpy as jnp
from jax import lax
from jax.sharding import PartitionSpec as P

NORM_EPS = 1e-5
ROPE_THETA = 500000.0


def rope_tables(seq_len, head_dim):
    half_dim = head_dim // 2
    inv_freq = 1.0 / (ROPE_THETA ** (jnp.arange(half_dim, dtype=jnp.float32) * 2.0 / head_dim))
    wavelen = 2.0 * math.pi / inv_freq
    smooth = (8192.0 / wavelen - 1.0) / 3.0
    scaled = jnp.where(wavelen > 8192.0, inv_freq / 8.0, (1.0 - smooth) * inv_freq / 8.0 + smooth * inv_freq)
    inv_freq = jnp.where(wavelen < 2048.0, inv_freq, scaled)
    angles = jnp.arange(seq_len, dtype=jnp.float32)[:, None] * inv_freq[None, :]
    return jnp.cos(angles), jnp.sin(angles)


def rotate(values, cos_t, sin_t):
    half_dim = values.shape[-1] // 2
    x_first = values[..., :half_dim]
    x_second = values[..., half_dim:]
    cos_b = cos_t[:, None, :]
    sin_b = sin_t[:, None, :]
    return jnp.concatenate([x_first * cos_b - x_second * sin_b, x_second * cos_b + x_first * sin_b], axis=-1)


def matmul(einsum_form, left_op, right_op):
    return jnp.einsum(einsum_form, left_op, right_op, preferred_element_type=jnp.float32)


def rms_forward(values, gain_vec):
    values32 = values.astype(jnp.float32)
    inv_rms = lax.rsqrt(jnp.mean(values32 * values32, axis=-1, keepdims=True) + NORM_EPS)
    normed = values32 * inv_rms
    return (normed * gain_vec.astype(jnp.float32)).astype(jnp.bfloat16), normed, inv_rms


def rms_backward(d_scaled, normed, inv_rms, gain_vec):
    d_scaled32 = d_scaled.astype(jnp.float32)
    d_gain = jnp.sum(d_scaled32 * normed, axis=(0, 1))
    d_normed = d_scaled32 * gain_vec.astype(jnp.float32)
    d_values = inv_rms * (d_normed - normed * jnp.mean(d_normed * normed, axis=-1, keepdims=True))
    return d_values, d_gain


def attention_forward(q_rot, k_rot, v_proj, doc_ids):
    seq_len, head_dim = q_rot.shape[1], q_rot.shape[-1]
    positions = jnp.arange(seq_len)
    allowed = (positions[:, None] >= positions[None, :])[None] & (doc_ids[:, :, None] == doc_ids[:, None, :])
    scores = matmul("bqgrd,bkgd->bgrqk", q_rot, k_rot) * head_dim ** -0.5
    attn_probs = jax.nn.softmax(jnp.where(allowed[:, None, None], scores, -1e30), axis=-1)
    probs_bf = attn_probs.astype(jnp.bfloat16)
    attn_heads = matmul("bgrqk,bkgd->bqgrd", probs_bf, v_proj).astype(jnp.bfloat16)
    return attn_heads, attn_probs, probs_bf


def attention_backward(d_attn, q_rot, k_rot, v_proj, attn_probs, probs_bf):
    head_dim = q_rot.shape[-1]
    d_v = matmul("bgrqk,bqgrd->bkgd", probs_bf, d_attn)
    d_probs = matmul("bqgrd,bkgd->bgrqk", d_attn, v_proj)
    d_scores = attn_probs * (d_probs - jnp.sum(d_probs * attn_probs, axis=-1, keepdims=True)) * head_dim ** -0.5
    d_scores = d_scores.astype(jnp.bfloat16)
    d_q_rot = matmul("bgrqk,bkgd->bqgrd", d_scores, k_rot)
    d_k_rot = matmul("bgrqk,bqgrd->bkgd", d_scores, q_rot)
    return d_q_rot, d_k_rot, d_v


def solution(mesh):
    def device_step(tokens, doc_ids, embedding, attn_norm, w_q, w_k, w_v, w_o, mlp_norm, w_gate, w_up, w_down, d_out):
        n_rows, seq_len = tokens.shape
        vocab_local, model_dim = embedding.shape
        heads_local, head_dim = w_q.shape[1], w_q.shape[2]
        kv_local = w_k.shape[1]
        group_size = heads_local // kv_local
        cos_t, sin_t = rope_tables(seq_len, head_dim)

        local_ids = tokens - lax.axis_index("tp") * vocab_local
        in_range = (local_ids >= 0) & (local_ids < vocab_local)
        rows_found = jnp.take(embedding, jnp.clip(local_ids, 0, vocab_local - 1), axis=0)
        x_part = jnp.where(in_range[:, :, None], rows_found, jnp.zeros((), jnp.bfloat16))
        x_emb = lax.psum_scatter(x_part, "tp", scatter_dimension=1, tiled=True)

        h_one, normed_one, inv_one = rms_forward(x_emb, attn_norm)
        h_one_full = lax.all_gather(h_one, "tp", axis=1, tiled=True)
        q_proj = matmul("btd,dhe->bthe", h_one_full, w_q).astype(jnp.bfloat16)
        k_proj = matmul("btd,dhe->bthe", h_one_full, w_k).astype(jnp.bfloat16)
        v_proj = matmul("btd,dhe->bthe", h_one_full, w_v).astype(jnp.bfloat16)
        q_rot = rotate(q_proj.astype(jnp.float32), cos_t, sin_t).astype(jnp.bfloat16)
        q_rot = q_rot.reshape(n_rows, seq_len, kv_local, group_size, head_dim)
        k_rot = rotate(k_proj.astype(jnp.float32), cos_t, sin_t).astype(jnp.bfloat16)
        attn_heads, attn_probs, probs_bf = attention_forward(q_rot, k_rot, v_proj, doc_ids)
        attn_flat = attn_heads.reshape(n_rows, seq_len, heads_local, head_dim)
        attn_part = matmul("bthe,hed->btd", attn_flat, w_o).astype(jnp.bfloat16)
        x_mid = x_emb + lax.psum_scatter(attn_part, "tp", scatter_dimension=1, tiled=True)

        h_two, normed_two, inv_two = rms_forward(x_mid, mlp_norm)
        h_two_full = lax.all_gather(h_two, "tp", axis=1, tiled=True)
        gate_proj = matmul("btd,df->btf", h_two_full, w_gate).astype(jnp.bfloat16)
        up_proj = matmul("btd,df->btf", h_two_full, w_up).astype(jnp.bfloat16)
        gate_f32 = gate_proj.astype(jnp.float32)
        up_f32 = up_proj.astype(jnp.float32)
        gate_sig = jax.nn.sigmoid(gate_f32)
        gate_act = gate_f32 * gate_sig
        mid_act = (gate_act * up_f32).astype(jnp.bfloat16)
        down_part = matmul("btf,fd->btd", mid_act, w_down).astype(jnp.bfloat16)
        y_out = x_mid + lax.psum_scatter(down_part, "tp", scatter_dimension=1, tiled=True)

        d_out_full = lax.all_gather(d_out, "tp", axis=1, tiled=True)
        d_w_down = matmul("btf,btd->fd", mid_act, d_out_full)
        d_mid = matmul("btd,fd->btf", d_out_full, w_down)
        d_up = (d_mid * gate_act).astype(jnp.bfloat16)
        d_gate = (d_mid * up_f32 * gate_sig * (1.0 + gate_f32 * (1.0 - gate_sig))).astype(jnp.bfloat16)
        d_w_gate = matmul("btd,btf->df", h_two_full, d_gate)
        d_w_up = matmul("btd,btf->df", h_two_full, d_up)
        d_h_two_part = (matmul("btf,df->btd", d_gate, w_gate) + matmul("btf,df->btd", d_up, w_up)).astype(jnp.bfloat16)
        d_h_two = lax.psum_scatter(d_h_two_part, "tp", scatter_dimension=1, tiled=True)
        d_mid_norm, d_mlp_norm = rms_backward(d_h_two, normed_two, inv_two, mlp_norm)
        d_x_mid32 = d_out.astype(jnp.float32) + d_mid_norm
        d_x_mid = d_x_mid32.astype(jnp.bfloat16)

        d_x_mid_full = lax.all_gather(d_x_mid, "tp", axis=1, tiled=True)
        d_w_o = matmul("bthe,btd->hed", attn_flat, d_x_mid_full)
        d_attn = matmul("btd,hed->bthe", d_x_mid_full, w_o).astype(jnp.bfloat16)
        d_attn = d_attn.reshape(n_rows, seq_len, kv_local, group_size, head_dim)
        d_q_rot, d_k_rot, d_v = attention_backward(d_attn, q_rot, k_rot, v_proj, attn_probs, probs_bf)
        d_q = rotate(d_q_rot.reshape(n_rows, seq_len, heads_local, head_dim), cos_t, -sin_t).astype(jnp.bfloat16)
        d_k = rotate(d_k_rot, cos_t, -sin_t).astype(jnp.bfloat16)
        d_v = d_v.astype(jnp.bfloat16)
        d_w_q = matmul("btd,bthe->dhe", h_one_full, d_q)
        d_w_k = matmul("btd,bthe->dhe", h_one_full, d_k)
        d_w_v = matmul("btd,bthe->dhe", h_one_full, d_v)
        d_h_one_part = (matmul("bthe,dhe->btd", d_q, w_q) + matmul("bthe,dhe->btd", d_k, w_k) + matmul("bthe,dhe->btd", d_v, w_v)).astype(jnp.bfloat16)
        d_h_one = lax.psum_scatter(d_h_one_part, "tp", scatter_dimension=1, tiled=True)
        d_emb_norm, d_attn_norm = rms_backward(d_h_one, normed_one, inv_one, attn_norm)
        d_x_emb = (d_x_mid32 + d_emb_norm).astype(jnp.bfloat16)

        d_x_full = lax.all_gather(d_x_emb, "tp", axis=1, tiled=True)
        seg_ids = jnp.where(in_range, local_ids, vocab_local).reshape(-1)
        d_embedding = jax.ops.segment_sum(d_x_full.reshape(-1, model_dim).astype(jnp.float32), seg_ids, num_segments=vocab_local)
        d_attn_norm = lax.psum(d_attn_norm, "tp")
        d_mlp_norm = lax.psum(d_mlp_norm, "tp")
        return (y_out, d_embedding, d_attn_norm, d_w_q, d_w_k, d_w_v, d_w_o, d_mlp_norm, d_w_gate, d_w_up, d_w_down)

    in_specs = (P("dp", None), P("dp", None), P("tp", None), P(None), P(None, "tp", None), P(None, "tp", None),
                P(None, "tp", None), P("tp", None, None), P(None), P(None, "tp"), P(None, "tp"), P("tp", None),
                P("dp", "tp", None))
    out_specs = (P("dp", "tp", None), P(("dp", "tp"), None), P("dp"), P("dp", "tp", None), P("dp", "tp", None),
                 P("dp", "tp", None), P(("dp", "tp"), None, None), P("dp"), P("dp", "tp"), P("dp", "tp"),
                 P(("dp", "tp"), None))
    return jax.shard_map(device_step, mesh=mesh, in_specs=in_specs, out_specs=out_specs, check_vma=False)
```

profile of v0, /device:TPU:0, one launch (start us, length us, event | category | flops | bytes accessed | tf_op | source)
XLA Modules:
  0.0 1446.6 jit_solution(17986182082693639404)
XLA Ops:
  8.2 68.5 %gather_fusion = bf16[2048,2048]{1,0:T(8,128)(2,1)} fusion(bf16[8000,2048]{1,0:T(8,128)(2,1)} %param.15, s32[2048]{0:T(1024)S(1)} %broadcast_clamp_fusion.1), kind=kCustom, calls=%fused_computation | custom fusion | bytes 16785408 | tf_op jit(solution)/shard_map/jit(_take)/gather | solution.py:83
  85.1 100.8 %reduce-scatter.6.cloned.1.call-done = bf16[1,512,2048]{2,1,0:T(8,128)(2,1)} async-done(((bf16[1,2048,2048]{2,1,0:T(8,128)(2,1)}), bf16[1,512,2048]{2,1,0:T(8,128)(2,1)}) %reduce-scatter.6.cloned.1.call-update) | async-done | bytes 2097168 | tf_op jit(solution)/shard_map/reduce_scatter | solution.py:85
  199.0 48.4 %all-gather.6.cloned.1.call-done = bf16[1,2048,2048]{2,1,0:T(8,128)(2,1)} async-done(((bf16[1,512,2048]{2,1,0:T(8,128)(2,1)}), bf16[1,2048,2048]{2,1,0:T(8,128)(2,1)}) %all-gather.6.cloned.1.call-update) | async-done | bytes 8388624 | tf_op jit(solution)/shard_map/all_gather | solution.py:88
  262.3 43.4 %fusion.7 = (f32[8,2048]{1,0:T(8,128)S(1)}, f32[2048,2048,8]{1,0,2:T(8,128)}) fusion(pred[2048,2048]{0,1:T(8,128)(4,1)S(1)} %copy-done.3, bf16[2048,8,32]{0,2,1:T(8,128)(2,1)S(1)} %get-tuple-element.26, bf16[2048,8,32]{0,2,1:T(8,128)(2,1)S(1)} %get-tuple-element.25, bf16[2048,32]{0,1:T(8,128)(2,1)S(1)} %get-tuple-element.30, ...), kind=kOutput, calls=%fused_computation.13 | convolution fusion | flops 4400332800 | bytes 140836864 | tf_op jit(solution)/shard_map/bqgrd,bkgd->bgrqk/dot_general | solution.py:32
  305.7 42.6 %fusion.6 = f32[8,2048]{1,0:T(8,128)S(1)} fusion(f32[2048,2048,8]{1,0,2:T(8,128)} %get-tuple-element.36, f32[8,2048]{1,0:T(8,128)S(1)} %get-tuple-element.35, pred[2048,2048]{0,1:T(8,128)(4,1)} %fusion.21), kind=kLoop, calls=%fused_computation.12 | loop fusion | flops 134201344 | bytes 138543104 | tf_op jit(solution)/shard_map/reduce_sum | solution.py:55
  354.6 49.5 %fusion.95 = bf16[2048,8,64]{0,2,1:T(8,128)(2,1)} fusion(bf16[2048,64,1]{0,1,2:T(8,128)(2,1)S(1)} %fusion.125, f32[8,2048]{1,0:T(8,128)S(1)} %fusion.6, f32[8,2048]{1,0:T(8,128)S(1)} %get-tuple-element.35, f32[2048,2048,8]{1,0,2:T(8,128)} %get-tuple-element.36, pred[2048,2048]{0,1:T(8,128)(4,1)S(1)} %copy-done.4), kind=kOutput, calls=%fused_computation.113 | convolution fusion | flops 4463788032 | bytes 140902400 | tf_op jit(solution)/shard_map/bgrqk,bkgd->bqgrd/dot_general | solution.py:32
  413.3 64.6 %reduce-scatter.8.cloned.1.call-done = bf16[1,512,2048]{2,1,0:T(8,128)(2,1)} async-done(((bf16[1,2048,2048]{2,1,0:T(8,128)(2,1)}), bf16[1,512,2048]{2,1,0:T(8,128)(2,1)}) %reduce-scatter.8.cloned.1.call-update) | async-done | bytes 2097168 | tf_op jit(solution)/shard_map/reduce_scatter | solution.py:98
  484.9 55.2 %all-gather.8.cloned.1.call-done = bf16[1,2048,2048]{2,1,0:T(8,128)(2,1)} async-done(((bf16[1,512,2048]{2,1,0:T(8,128)(2,1)}), bf16[1,2048,2048]{2,1,0:T(8,128)(2,1)}) %all-gather.8.cloned.1.call-update) | async-done | bytes 8388624 | tf_op jit(solution)/shard_map/all_gather | solution.py:101
  540.2 19.0 %fusion.60 = bf16[2048,1408]{1,0:T(8,128)(2,1)} fusion(bf16[2048,1408]{1,0:T(8,128)(2,1)} %param.22, bf16[1,2048,2048]{2,1,0:T(8,128)(2,1)} %all-gather.8.cloned.1.call-done), kind=kOutput, calls=%fused_computation.77 | convolution fusion | flops 11814043648 | bytes 19922944 | tf_op jit(solution)/shard_map/btd,df->btf/dot_general | solution.py:32
  559.1 17.0 %fusion.63 = bf16[2048,1408]{1,0:T(8,128)(2,1)} fusion(bf16[2048,1408]{1,0:T(8,128)(2,1)} %param.23, bf16[1,2048,2048]{2,1,0:T(8,128)(2,1)S(1)} %copy-done.45), kind=kOutput, calls=%fused_computation.78 | convolution fusion | flops 11814043648 | bytes 19922944 | tf_op jit(solution)/shard_map/btd,df->btf/dot_general | solution.py:32
  576.1 21.2 %all-gather.10.cloned.1.call-done = bf16[1,2048,2048]{2,1,0:T(8,128)(2,1)} async-done(((bf16[1,512,2048]{2,1,0:T(8,128)(2,1)}), bf16[1,2048,2048]{2,1,0:T(8,128)(2,1)}) %all-gather.10.cloned.1.call-update) | async-done | bytes 8388624 | tf_op jit(solution)/shard_map/all_gather | solution.py:112
  597.3 25.8 %fusion.25 = (bf16[2048,1408]{1,0:T(8,128)(2,1)}, f32[2048,1408]{1,0:T(8,128)}) fusion(bf16[2048,1408]{1,0:T(8,128)(2,1)} %fusion.63, bf16[2048,1408]{1,0:T(8,128)(2,1)} %fusion.60, bf16[1408,2048]{1,0:T(8,128)(2,1)} %param.24, bf16[1,2048,2048]{2,1,0:T(8,128)(2,1)} %all-gather.10.cloned.1.call-done), kind=kOutput, calls=%fused_computation.38 | convolution fusion | flops 11845763072 | bytes 42991616 | tf_op jit(solution)/shard_map/btd,fd->btf/dot_general | solution.py:32
  623.1 19.4 %fusion.160 = f32[2048,2048]{1,0:T(8,128)} fusion(bf16[2048,1408]{1,0:T(8,128)(2,1)} %get-tuple-element.37, bf16[2048,1408]{1,0:T(8,128)(2,1)} %param.22), kind=kOutput, calls=%fused_computation.181 | convolution fusion | flops 11811160064 | bytes 28311552 | tf_op jit(solution)/shard_map/btf,df->btd/dot_general | solution.py:32
  642.5 22.3 %fusion.30 = bf16[1,2048,2048]{2,1,0:T(8,128)(2,1)} fusion(f32[2048,2048]{1,0:T(8,128)} %fusion.160, bf16[2048,1408]{1,0:T(8,128)(2,1)} %param.23, f32[2048,1408]{1,0:T(8,128)} %get-tuple-element.38, bf16[2048,1408]{1,0:T(8,128)(2,1)} %fusion.60), kind=kOutput, calls=%fused_computation.44 | convolution fusion | flops 11839733760 | bytes 48234496 | tf_op jit(solution)/shard_map/btf,df->btd/dot_general | solution.py:32
  664.9 65.2 %reduce-scatter.12.cloned.1.call-done = bf16[1,512,2048]{2,1,0:T(8,128)(2,1)} async-done(((bf16[1,2048,2048]{2,1,0:T(8,128)(2,1)}), bf16[1,512,2048]{2,1,0:T(8,128)(2,1)}) %reduce-scatter.12.cloned.1.call-update) | async-done | bytes 2097168 | tf_op jit(solution)/shard_map/reduce_scatter | solution.py:120
  740.5 55.8 %all-gather.12.cloned.1.call-done = bf16[1,2048,2048]{2,1,0:T(8,128)(2,1)} async-done(((bf16[1,512,2048]{2,1,0:T(8,128)(2,1)}), bf16[1,2048,2048]{2,1,0:T(8,128)(2,1)}) %all-gather.12.cloned.1.call-update) | async-done | bytes 8388624 | tf_op jit(solution)/shard_map/all_gather | solution.py:125
  796.3 9.8 fusion.92
  806.1 48.3 %fusion.116 = bf16[2048,64]{0,1:T(8,128)(2,1)} fusion(bf16[2048,8,64]{0,2,1:T(8,128)(2,1)} %fusion.92, f32[8,2048]{1,0:T(8,128)S(1)} %copy-done.28, f32[8,2048]{1,0:T(8,128)S(1)} %copy-done.26, f32[2048,2048,8]{1,0,2:T(8,128)} %get-tuple-element.36, pred[2048,2048]{0,1:T(8,128)(4,1)} %fusion.21), kind=kOutput, calls=%fused_computation.121 | convolution fusion | flops 4462870528 | bytes 140902400 | tf_op jit(solution)/shard_map/bgrqk,bqgrd->bkgd/dot_general | solution.py:32
  854.4 103.0 %fusion.1 = (f32[8,2048]{1,0:T(8,128)S(1)}, f32[2048,2048,8]{1,0,2:T(8,128)}) fusion(f32[8,2048]{1,0:T(8,128)S(1)} %copy-done.28, f32[8,2048]{1,0:T(8,128)S(1)} %copy-done.26, f32[2048,2048,8]{1,0,2:T(8,128)} %get-tuple-element.36, pred[2048,2048]{0,1:T(8,128)(4,1)} %fusion.21, bf16[2048,64,1]{0,1,2:T(8,128)(2,1)S(1)} %copy-done.24, ...), kind=kOutput, calls=%fused_computation.6 | convolution fusion | flops 4496277504 | bytes 275185664 | tf_op jit(solution)/shard_map/bqgrd,bkgd->bgrqk/dot_general | solution.py:32
  957.4 105.8 %fusion.8 = bf16[8,2048,2048]{1,2,0:T(8,128)(2,1)} fusion(f32[2048,2048,8]{1,0,2:T(8,128)} %get-tuple-element.40, f32[8,2048]{1,0:T(8,128)S(1)} %get-tuple-element.39, f32[8,2048]{1,0:T(8,128)S(1)} %copy-done.28, f32[8,2048]{1,0:T(8,128)S(1)} %copy-done.26, f32[2048,2048,8]{1,0,2:T(8,128)} %get-tuple-element.36, pred[2048,2048]{0,1:T(8,128)(4,1)} %fusion.21), kind=kLoop, calls=%fused_computation.14 | loop fusion | flops 268435456 | bytes 339935232 | tf_op jit(solution)/shard_map/reshape.71
  1063.2 30.9 %convolution_bitcast_fusion.1 = f32[1,2048,1,64]{1,3,2,0:T(8,128)} fusion(bf16[8,2048,2048]{1,2,0:T(8,128)(2,1)} %fusion.8, bf16[2048,8,32]{0,2,1:T(8,128)(2,1)} %copy-done.7, bf16[2048,8,32]{0,2,1:T(8,128)(2,1)S(1)} %copy-done.6), kind=kOutput, calls=%fused_computation.117 | convolution fusion | flops 4299161600 | bytes 69730304 | tf_op jit(solution)/shard_map/bgrqk,bqgrd->bkgd/dot_general | solution.py:32
  1094.1 23.7 %convolution_bitcast_fusion = f32[1,2048,8,64]{1,3,2,0:T(8,128)S(1)} fusion(bf16[8,2048,2048]{1,2,0:T(8,128)(2,1)} %fusion.8, bf16[2048,32]{0,1:T(8,128)(2,1)} %copy-done.22, bf16[2048,32]{0,1:T(8,128)(2,1)S(1)} %copy-done.21), kind=kOutput, calls=%fused_computation.110 | convolution fusion | flops 4295491584 | bytes 71565312 | tf_op jit(solution)/shard_map/bgrqk,bkgd->bqgrd/dot_general | solution.py:32
  1128.0 8.5 fusion.134
  1136.5 15.4 %fusion.67 = bf16[1,2048,2048]{2,1,0:T(8,128)(2,1)} fusion(bf16[2048,64]{0,1:T(8,128)(2,1)S(1)} %copy-done.12, f32[2048,2048]{1,0:T(8,128)} %fusion.134, f32[2048,2048,1]{1,0,2:T(8,128)} %fusion.155, bf16[2048,1,64]{0,2,1:T(8,128)(2,1)} %param.19), kind=kOutput, calls=%fused_computation.80 | convolution fusion | flops 549453824 | bytes 42467328 | tf_op jit(solution)/shard_map/bthe,dhe->btd/dot_general | solution.py:32
  1152.0 20.6 %convert_bitcast_fusion = bf16[1,2048,2048]{2,1,0:T(8,128)(2,1)} fusion(bf16[1408,2048]{1,0:T(8,128)(2,1)} %param.24, bf16[2048,1408]{1,0:T(8,128)(2,1)} %fusion.63, bf16[2048,1408]{1,0:T(8,128)(2,1)} %fusion.60), kind=kOutput, calls=%fused_computation.76 | convolution fusion | flops 11838423040 | bytes 25690112 | tf_op jit(solution)/shard_map/btf,fd->btd/dot_general | solution.py:32
  1181.7 35.6 %reduce-scatter.14.cloned.1.call-done = bf16[1,512,2048]{2,1,0:T(8,128)(2,1)} async-done(((bf16[1,2048,2048]{2,1,0:T(8,128)(2,1)}), bf16[1,512,2048]{2,1,0:T(8,128)(2,1)}) %reduce-scatter.14.cloned.1.call-update) | async-done | bytes 2097168 | tf_op jit(solution)/shard_map/reduce_scatter | solution.py:137
  1228.3 18.9 %fusion.41 = f32[2048,1408]{1,0:T(8,128)} fusion(bf16[2048,1408]{1,0:T(8,128)(2,1)} %get-tuple-element.37, bf16[1,2048,2048]{2,1,0:T(8,128)(2,1)} %all-gather.8.cloned.1.call-done), kind=kOutput, calls=%fused_computation.56 | convolution fusion | flops 11811160064 | bytes 25690112 | tf_op jit(solution)/shard_map/btd,btf->df/dot_general | solution.py:32
  1247.2 23.0 %fusion.35 = f32[1408,2048]{1,0:T(8,128)} fusion(bf16[1,2048,2048]{2,1,0:T(8,128)(2,1)} %all-gather.10.cloned.1.call-done, bf16[2048,1408]{1,0:T(8,128)(2,1)} %fusion.63, bf16[2048,1408]{1,0:T(8,128)(2,1)} %fusion.60), kind=kOutput, calls=%fused_computation.50 | convolution fusion | flops 11834228736 | bytes 31457280 | tf_op jit(solution)/shard_map/btf,btd->fd/dot_general | solution.py:32
  1270.2 30.4 %fusion.39 = f32[2048,1408]{1,0:T(8,128)} fusion(bf16[1,2048,2048]{2,1,0:T(8,128)(2,1)S(1)} %bitcast.256, f32[2048,1408]{1,0:T(8,128)} %get-tuple-element.38, bf16[2048,1408]{1,0:T(8,128)(2,1)S(1)} %bitcast.261), kind=kOutput, calls=%fused_computation.54 | convolution fusion | flops 11831345152 | bytes 37224448 | tf_op jit(solution)/shard_map/btd,btf->df/dot_general | solution.py:32
  1326.5 11.9 all-reduce
  1342.9 11.3 bitcast_convert_fusion.1
  1354.2 85.1 %scatter_custom_fusion = f32[8000,2048]{1,0:T(8,128)} fusion(s32[2048]{0:T(1024)} %get-tuple-element.11, f32[]{:T(128)} %constant.27.clone.1, f32[2048,2048]{1,0:T(8,128)} %bitcast_convert_fusion.1, s32[2048]{0:T(1024)} %broadcast_clamp_fusion), kind=kCustom, calls=%fused_computation.20 | custom fusion | flops 4194304 | bytes 65536512 | tf_op jit(solution)/shard_map/scatter-add | solution.py:143
  (178 shorter events, 130.4 us)
Async XLA Ops:
  7.2 247.6 %copy-start = (bf16[2048,8,64]{0,2,1:T(8,128)(2,1)S(1)}, bf16[2048,8,64]{0,2,1:T(8,128)(2,1)}, u32[]{:S(2)}) copy-start(bf16[2048,8,64]{0,2,1:T(8,128)(2,1)} %param.17) | copy-start | bytes 6291460
  7.2 178.7 %reduce-scatter.6.cloned.1.call-start = ((), (), s32[]{:S(2)}) async-start(), calls=%async_computation.5 | async-start | bytes 10485760 | tf_op jit(solution)/shard_map/reduce_scatter | solution.py:85
  84.5 109.2 %copy-start.36 = (s32[1,2048]{1,0:T(1,128)S(1)}, s32[1,2048]{1,0:T(1,128)}, u32[]{:S(2)}) copy-start(s32[1,2048]{1,0:T(1,128)} %param.14) | copy-start | bytes 24580
  84.5 163.0 %all-gather.6.cloned.1.call-start = ((), (), s32[]{:S(2)}) async-start(), calls=%async_computation.6 | async-start | bytes 10485760 | tf_op jit(solution)/shard_map/all_gather | solution.py:88
  85.1 106.7 %copy-start.32 = (f32[2048]{0:T(1024)}, f32[2048]{0:T(1024)S(1)}, u32[]{:S(2)}) copy-start(f32[2048]{0:T(1024)S(1)} %convert_element_type.167) | copy-start | bytes 24580
  188.0 59.4 %copy-start.16 = (bf16[2048,1,64]{0,2,1:T(8,128)(2,1)S(1)}, bf16[2048,1,64]{0,2,1:T(8,128)(2,1)}, u32[]{:S(2)}) copy-start(bf16[2048,1,64]{0,2,1:T(8,128)(2,1)} %param.18) | copy-start | bytes 786436
  191.5 286.3 %reduce-scatter.8.cloned.1.call-start = ((), (), s32[]{:S(2)}) async-start(), calls=%async_computation.7 | async-start | bytes 10485760 | tf_op jit(solution)/shard_map/reduce_scatter | solution.py:98
  191.8 61.8 %copy-start.41 = (f32[32]{0:T(128)}, f32[32]{0:T(128)S(1)}, u32[]{:S(2)}) copy-start(f32[32]{0:T(128)S(1)} %compare_select_fusion.2) | copy-start | bytes 388
  193.6 66.0 %copy-start.10 = (f32[2048,32]{0,1:T(8,128)}, f32[2048,32]{0,1:T(8,128)S(1)}, u32[]{:S(2)}) copy-start(f32[2048,32]{0,1:T(8,128)S(1)} %get-tuple-element.34) | copy-start | bytes 786436
  260.3 45.4 %copy-start.5 = (bf16[2048,8,32]{0,2,1:T(8,128)(2,1)}, bf16[2048,8,32]{0,2,1:T(8,128)(2,1)S(1)}, u32[]{:S(2)}) copy-start(bf16[2048,8,32]{0,2,1:T(8,128)(2,1)S(1)} %get-tuple-element.25) | copy-start | bytes 3145732
  260.3 45.4 %copy-start.7 = (bf16[2048,8,32]{0,2,1:T(8,128)(2,1)}, bf16[2048,8,32]{0,2,1:T(8,128)(2,1)S(1)}, u32[]{:S(2)}) copy-start(bf16[2048,8,32]{0,2,1:T(8,128)(2,1)S(1)} %get-tuple-element.26) | copy-start | bytes 3145732
  305.7 48.8 %copy-start.25 = (f32[8,2048]{1,0:T(8,128)}, f32[8,2048]{1,0:T(8,128)S(1)}, u32[]{:S(2)}) copy-start(f32[8,2048]{1,0:T(8,128)S(1)} %get-tuple-element.35) | copy-start | bytes 196612
  305.7 42.6 %copy-start.19 = (bf16[2048,1,64]{0,2,1:T(8,128)(2,1)S(1)}, bf16[2048,1,64]{0,2,1:T(8,128)(2,1)}, u32[]{:S(2)}) copy-start(bf16[2048,1,64]{0,2,1:T(8,128)(2,1)} %param.19) | copy-start | bytes 786436
  354.6 49.5 %copy-start.23 = (bf16[2048,64,1]{0,1,2:T(8,128)(2,1)}, bf16[2048,64,1]{0,1,2:T(8,128)(2,1)S(1)}, u32[]{:S(2)}) copy-start(bf16[2048,64,1]{0,1,2:T(8,128)(2,1)S(1)} %fusion.125) | copy-start | bytes 786436
  354.6 49.5 %copy-start.46 = (bf16[8,64,2048]{2,1,0:T(8,128)(2,1)S(1)}, bf16[8,64,2048]{2,1,0:T(8,128)(2,1)}, u32[]{:S(2)}) copy-start(bf16[8,64,2048]{2,1,0:T(8,128)(2,1)} %param.20) | copy-start | bytes 6291460
  412.6 127.6 %all-gather.8.cloned.1.call-start = ((), (), s32[]{:S(2)}) async-start(), calls=%async_computation.8 | async-start | bytes 10485760 | tf_op jit(solution)/shard_map/all_gather | solution.py:101
  413.3 71.0 %copy-start.29 = (f32[2048]{0:T(1024)}, f32[2048]{0:T(1024)S(1)}, u32[]{:S(2)}) copy-start(f32[2048]{0:T(1024)S(1)} %convert_element_type.183) | copy-start | bytes 24580
  484.3 113.0 %all-gather.10.cloned.1.call-start = ((), (), s32[]{:S(2)}) async-start(), calls=%async_computation.10 | async-start | bytes 10485760 | tf_op jit(solution)/shard_map/all_gather | solution.py:112
  484.9 245.1 %reduce-scatter.12.cloned.1.call-start = ((), (), s32[]{:S(2)}) async-start(), calls=%async_computation.11 | async-start | bytes 10485760 | tf_op jit(solution)/shard_map/reduce_scatter | solution.py:120
  664.8 65.3 %copy-start.30 = (f32[2048]{0:T(1024)S(1)}, f32[2048]{0:T(1024)}, u32[]{:S(2)}) copy-start(f32[2048]{0:T(1024)} %copy-done.29) | copy-start | bytes 24580
  664.8 65.3 %copy-start.35 = (f32[512]{0:T(512)S(1)}, f32[512]{0:T(512)}, u32[]{:S(2)}) copy-start(f32[512]{0:T(512)} %copy-done.34) | copy-start | bytes 6148
  664.8 131.5 %all-gather.12.cloned.1.call-start = ((), (), s32[]{:S(2)}) async-start(), calls=%async_computation.12 | async-start | bytes 10485760 | tf_op jit(solution)/shard_map/all_gather | solution.py:125
  740.4 65.7 %copy-start.26 = (f32[8,2048]{1,0:T(8,128)S(1)}, f32[8,2048]{1,0:T(8,128)}, u32[]{:S(2)}) copy-start(f32[8,2048]{1,0:T(8,128)} %copy-done.25) | copy-start | bytes 196612
  740.4 65.7 %copy-start.28 = (f32[8,2048]{1,0:T(8,128)S(1)}, f32[8,2048]{1,0:T(8,128)}, u32[]{:S(2)}) copy-start(f32[8,2048]{1,0:T(8,128)} %copy-done.27) | copy-start | bytes 196612
  740.4 476.8 %reduce-scatter.14.cloned.1.call-start = ((), (), s32[]{:S(2)}) async-start(), calls=%async_computation.13 | async-start | bytes 10485760 | tf_op jit(solution)/shard_map/reduce_scatter | solution.py:137
  806.1 48.3 %copy-start.24 = (bf16[2048,64,1]{0,1,2:T(8,128)(2,1)S(1)}, bf16[2048,64,1]{0,1,2:T(8,128)(2,1)}, u32[]{:S(2)}) copy-start(bf16[2048,64,1]{0,1,2:T(8,128)(2,1)} %copy-done.23) | copy-start | bytes 786436
  957.4 105.8 %copy-start.6 = (bf16[2048,8,32]{0,2,1:T(8,128)(2,1)S(1)}, bf16[2048,8,32]{0,2,1:T(8,128)(2,1)}, u32[]{:S(2)}) copy-start(bf16[2048,8,32]{0,2,1:T(8,128)(2,1)} %copy-done.5) | copy-start | bytes 3145732
  1152.0 148.7 %reduce-scatter.10.cloned.1.call-start = ((), (), s32[]{:S(2)}) async-start(), calls=%async_computation.9 | async-start | bytes 10485760 | tf_op jit(solution)/shard_map/reduce_scatter | solution.py:110
  1172.7 44.6 %copy-start.33 = (f32[2048]{0:T(1024)S(1)}, f32[2048]{0:T(1024)}, u32[]{:S(2)}) copy-start(f32[2048]{0:T(1024)} %copy-done.32) | copy-start | bytes 24580
  1172.7 48.8 %copy-start.31 = (f32[2048]{0:T(1024)S(1)}, f32[2048]{0:T(1024)}, u32[]{:S(2)}) copy-start(f32[2048]{0:T(1024)} %copy-done.29) | copy-start | bytes 24580
  1172.7 170.2 %all-gather.14.cloned.1.call-start = ((), (), s32[]{:S(2)}) async-start(), calls=%async_computation.14 | async-start | bytes 10485760 | tf_op jit(solution)/shard_map/all_gather | solution.py:141
  1228.3 41.9 %slice-start.2 = ((s8[8388608]{0:T(1024)(128)(4,1)}), s8[4194304]{0:T(1024)(128)(4,1)S(1)}, s32[]{:S(2)}) async-start(s8[8388608]{0:T(1024)(128)(4,1)} %bitcast.255), calls=%async_computation.17 | async-start | bytes 8388608
  (34 other events, 363.3 us)
Sparse Core Ops, SparseCore 0:
  84.6 101.2 reduce-scatter.5
  191.7 55.7 all-gather.5
  412.7 65.0 reduce-scatter.7
  484.4 55.7 all-gather.7
  541.5 55.7 all-gather.9
  664.9 65.0 reduce-scatter.11
  740.5 55.7 all-gather.11
  1152.1 65.1 reduce-scatter.13
  1220.4 65.0 reduce-scatter.9
  1286.9 55.9 all-gather.13
where the time goes:
time: 1450 us
  matrix products  583 us (40%)
  waiting for transfers between devices  452 us (31%)
  other arithmetic  309 us (21%)
  local copies, waits for them, and re-layouts  75 us (5%)
  between operations  15.2 us (1%)
    dot_general x25, matrix products, matmul(): jnp.einsum(einsum_form, left_op, right_op, preferred_element_type=jnp.flo...  572 us
    another operation x1, other arithmetic  106 us
    reduce_scatter x1, waiting for transfers between devices, device_step(): x_emb = lax.psum_scatter(x_part, 'tp', scatter_dimension=1, tiled=True)  101 us
    scatter-add x3, other arithmetic, device_step(): jax.ops.segment_sum(d_x_full.reshape(-1, model_dim).astype(jnp.float32),...  92.2 us
    gather x1, local copies, waits for them, and re-layouts, device_step(): jnp.take(embedding, jnp.clip(local_ids, 0, vocab_local - 1), axis=0)  68.5 us
    reduce_scatter x1, waiting for transfers between devices, device_step(): lax.psum_scatter(d_h_two_part, 'tp', scatter_dimension=1, tiled=True)  65.2 us
    reduce_scatter x1, waiting for transfers between devices, device_step(): lax.psum_scatter(attn_part, 'tp', scatter_dimension=1, tiled=True)  64.6 us
    all_gather x1, waiting for transfers between devices, device_step(): d_x_mid_full = lax.all_gather(d_x_mid, 'tp', axis=1, tiled=True)  55.8 us
  transfers between devices with their start and end apart: 10, of which 9 were waited for; matrix products, arithmetic and copies ran while one was open for 13% of the time, Pallas kernels for 0%

commit v1 on v0

v1 whole, which is shorter than its diff:
```python
import functools
import math
import jax
import jax.numpy as jnp
from jax import lax
from jax.experimental import pallas as pl
from jax.experimental.pallas import tpu as pltpu
from jax.sharding import PartitionSpec as P

NORM_EPS = 1e-5
ROPE_THETA = 500000.0
BQ = 256
BK = 256
HEADS = 8
HD = 64
HALF = HD // 2
LOG2E = 1.4426950408889634
SCALE2 = LOG2E * HD ** -0.5
NEG = -1e30
ROWS_OUT = 200
F32 = jnp.float32
BF16 = jnp.bfloat16


def rope_tables_t(positions):
    inv_freq = 1.0 / (ROPE_THETA ** (jnp.arange(HALF, dtype=F32) * 2.0 / HD))
    wavelen = 2.0 * math.pi / inv_freq
    smooth = (8192.0 / wavelen - 1.0) / 3.0
    scaled = jnp.where(wavelen > 8192.0, inv_freq / 8.0, (1.0 - smooth) * inv_freq / 8.0 + smooth * inv_freq)
    inv_freq = jnp.where(wavelen < 2048.0, inv_freq, scaled)
    angles = inv_freq[:, None] * positions.astype(F32)[None, :]
    return jnp.cos(angles), jnp.sin(angles)


def dot(a, b, ca, cb):
    return lax.dot_general(a, b, (((ca,), (cb,)), ((), ())), preferred_element_type=F32)


def rms_forward(values, gain_vec):
    values32 = values.astype(F32)
    inv_rms = lax.rsqrt(jnp.mean(values32 * values32, axis=-1, keepdims=True) + NORM_EPS)
    return (values32 * inv_rms * gain_vec.astype(F32)).astype(BF16), inv_rms


def rms_backward(d_scaled32, values, inv_rms, gain_vec):
    normed = values.astype(F32) * inv_rms
    d_gain = jnp.sum(d_scaled32 * normed, axis=0)
    d_normed = d_scaled32 * gain_vec.astype(F32)
    d_values = inv_rms * (d_normed - normed * jnp.mean(d_normed * normed, axis=-1, keepdims=True))
    return d_values, d_gain


def rel_col(block, shard_bits, block_size):
    per = 512 // block_size
    return pl.multiple_of(((block // per) ^ shard_bits) * 512 + (block % per) * block_size, block_size)


def rope_keys(kv_ref, cos_ref, sin_ref):
    k1 = kv_ref[0:HALF, :].astype(F32)
    k2 = kv_ref[HALF:HD, :].astype(F32)
    cos_v = cos_ref[...]
    sin_v = sin_ref[...]
    return jnp.concatenate([k1 * cos_v - k2 * sin_v, k2 * cos_v + k1 * sin_v], axis=0)


def key_bias(kblk, qblk, qs_row):
    kpos = kblk * BK + lax.broadcasted_iota(jnp.int32, (BK, BQ), 0)
    qpos = qblk * BQ + lax.broadcasted_iota(jnp.int32, (BK, BQ), 1)
    return jnp.where((kpos <= qpos) & (kpos >= qs_row), 0.0, NEG)


def attn_fwd_kernel(start, s_ref, q_ref, kv_ref, cos_ref, sin_ref, qs_ref, o_ref, qr_ref, lse_ref,
                    k_scr, acc, m_scr, l_scr, bias):
    i = pl.program_id(0)
    me = s_ref[8]

    @pl.when(i == 0)
    def _():
        k_scr[...] = rope_keys(kv_ref, cos_ref, sin_ref).T.astype(BF16)

    rb = start + i
    qcol = pl.multiple_of(rb * BQ, BQ)
    ab = ((rb // 2) ^ me) * 2 + rb % 2
    cos_v = cos_ref[:, pl.ds(qcol, BQ)]
    sin_v = sin_ref[:, pl.ds(qcol, BQ)]
    qs_row = qs_ref[:, pl.ds(qcol, BQ)]
    for h in range(HEADS):
        q1 = q_ref[h * HD:h * HD + HALF, :].astype(F32)
        q2 = q_ref[h * HD + HALF:(h + 1) * HD, :].astype(F32)
        qr_ref[h * HD:h * HD + HALF, :] = (q1 * cos_v - q2 * sin_v).astype(BF16)
        qr_ref[h * HD + HALF:(h + 1) * HD, :] = (q2 * cos_v + q1 * sin_v).astype(BF16)
    acc[...] = jnp.zeros_like(acc)
    m_scr[...] = jnp.full_like(m_scr, NEG)
    l_scr[...] = jnp.zeros_like(l_scr)

    def step(j, carry):
        col = rel_col(j, me, BK)
        k_blk = k_scr[pl.ds(col, BK), :]
        v_blk = kv_ref[HD:2 * HD, pl.ds(col, BK)]
        bias[...] = key_bias(j, ab, qs_row)
        for h in range(HEADS):
            rows = slice(h * HD, (h + 1) * HD)
            s = dot(k_blk, qr_ref[rows, :], 1, 0) * SCALE2 + bias[...]
            m_old = m_scr[h:h + 1, :]
            m_new = jnp.maximum(m_old, jnp.max(s, axis=0, keepdims=True))
            p = jnp.exp2(s - m_new)
            alpha = jnp.exp2(m_old - m_new)
            l_scr[h:h + 1, :] = l_scr[h:h + 1, :] * alpha + jnp.sum(p, axis=0, keepdims=True)
            m_scr[h:h + 1, :] = m_new
            acc[rows, :] = acc[rows, :] * alpha + dot(v_blk, p.astype(BF16), 1, 0)
        return carry

    lax.fori_loop(s_ref[ab], ab + 1, step, 0)
    for h in range(HEADS):
        rows = slice(h * HD, (h + 1) * HD)
        o_ref[rows, :] = (acc[rows, :] / l_scr[h:h + 1, :]).astype(BF16)
    lse_ref[...] = m_scr[...] + jnp.log2(l_scr[...])


def attn_fwd(scal, qkv_t, cos_t, sin_t, qs_row, start, count):
    width = count * BQ
    whole = lambda i, s: (0, 0)
    return pl.pallas_call(
        functools.partial(attn_fwd_kernel, start),
        grid_spec=pltpu.PrefetchScalarGridSpec(
            num_scalar_prefetch=1,
            grid=(count,),
            in_specs=[
                pl.BlockSpec((HEADS * HD, BQ), lambda i, s: (0, start + i)),
                pl.BlockSpec((2 * HD, 2048), lambda i, s: (4, 0)),
                pl.BlockSpec((HALF, 2048), whole),
                pl.BlockSpec((HALF, 2048), whole),
                pl.BlockSpec((1, 2048), whole),
            ],
            out_specs=[
                pl.BlockSpec((HEADS * HD, BQ), lambda i, s: (0, i)),
                pl.BlockSpec((HEADS * HD, BQ), lambda i, s: (0, i)),
                pl.BlockSpec((HEADS, BQ), lambda i, s: (0, i)),
            ],
            scratch_shapes=[
                pltpu.VMEM((2048, HD), BF16),
                pltpu.VMEM((HEADS * HD, BQ), F32),
                pltpu.VMEM((HEADS, BQ), F32),
                pltpu.VMEM((HEADS, BQ), F32),
                pltpu.VMEM((BK, BQ), F32),
            ],
        ),
        out_shape=[
            jax.ShapeDtypeStruct((HEADS * HD, width), BF16),
            jax.ShapeDtypeStruct((HEADS * HD, width), BF16),
            jax.ShapeDtypeStruct((HEADS, width), F32),
        ],
        compiler_params=pltpu.CompilerParams(dimension_semantics=("arbitrary",), vmem_limit_bytes=48 << 20),
        cost_estimate=pl.CostEstimate(flops=int(10e9), bytes_accessed=8 << 20, transcendentals=0),
        name="attn_fwd",
    )(scal, qkv_t, qkv_t, cos_t, sin_t, qs_row)


def attn_bwd_kernel(start, last, s_ref, qr_ref, do_ref, o_ref, lse_ref, kv_ref, cos_ref, sin_ref, qs_ref, *rest):
    if last:
        dk_in, dv_in, dq_ref, dkv_ref, dk, dv, k_scr, kt_scr, v_scr, qcat, docat, delta, dq, bias, p_scr, ds_scr = rest
    else:
        dq_ref, dk, dv, k_scr, kt_scr, v_scr, qcat, docat, delta, dq, bias, p_scr, ds_scr = rest
    i = pl.program_id(0)
    me = s_ref[8]

    @pl.when(i == 0)
    def _():
        kt = rope_keys(kv_ref, cos_ref, sin_ref)
        kt_scr[...] = kt.astype(BF16)
        k_scr[...] = kt.T.astype(BF16)
        v_scr[...] = kv_ref[HD:2 * HD, :].astype(F32).T.astype(BF16)
        if last:
            dk[...] = dk_in[...]
            dv[...] = dv_in[...]
        else:
            dk[...] = jnp.zeros_like(dk)
            dv[...] = jnp.zeros_like(dv)

    rb = start + i
    qcol = pl.multiple_of(rb * BQ, BQ)
    ab = ((rb // 2) ^ me) * 2 + rb % 2
    qs_row = qs_ref[:, pl.ds(qcol, BQ)]
    for h in range(HEADS):
        rows = slice(h * HD, (h + 1) * HD)
        cols = slice(h * BQ, (h + 1) * BQ)
        do_h = do_ref[rows, :]
        qcat[:, cols] = qr_ref[rows, :]
        docat[:, cols] = do_h
        delta[h:h + 1, :] = jnp.sum(o_ref[rows, :].astype(F32) * do_h.astype(F32), axis=0, keepdims=True)
    dq[...] = jnp.zeros_like(dq)

    def step(j, carry):
        col = rel_col(j, me, BK)
        k_blk = k_scr[pl.ds(col, BK), :]
        v_blk = v_scr[pl.ds(col, BK), :]
        bias[...] = key_bias(j, ab, qs_row)
        for h in range(HEADS):
            cols = slice(h * BQ, (h + 1) * BQ)
            s = dot(k_blk, qcat[:, cols], 1, 0) * SCALE2 + bias[...]
            p = jnp.exp2(s - lse_ref[h:h + 1, :])
            d_p = dot(v_blk, docat[:, cols], 1, 0)
            p_scr[:, cols] = p.astype(BF16)
            ds_scr[:, cols] = (p * (d_p - delta[h:h + 1, :])).astype(BF16)
        dv[pl.ds(col, BK), :] += dot(p_scr[...], docat[...], 1, 1)
        dk[pl.ds(col, BK), :] += dot(ds_scr[...], qcat[...], 1, 1)
        dq[...] += dot(kt_scr[:, pl.ds(col, BK)], ds_scr[...], 1, 0)
        return carry

    lax.fori_loop(s_ref[ab], ab + 1, step, 0)
    cos_v = cos_ref[:, pl.ds(qcol, BQ)]
    sin_v = sin_ref[:, pl.ds(qcol, BQ)]
    for h in range(HEADS):
        cols = slice(h * BQ, (h + 1) * BQ)
        g1 = dq[0:HALF, cols] * HD ** -0.5
        g2 = dq[HALF:HD, cols] * HD ** -0.5
        dq_ref[h * HD:h * HD + HALF, :] = (g1 * cos_v + g2 * sin_v).astype(BF16)
        dq_ref[h * HD + HALF:(h + 1) * HD, :] = (g2 * cos_v - g1 * sin_v).astype(BF16)

    if last:
        @pl.when(i == pl.num_programs(0) - 1)
        def _():
            kt = dk[...].T * HD ** -0.5
            g1 = kt[0:HALF, :]
            g2 = kt[HALF:HD, :]
            cos_a = cos_ref[...]
            sin_a = sin_ref[...]
            dkv_ref[0:HALF, :] = (g1 * cos_a + g2 * sin_a).astype(BF16)
            dkv_ref[HALF:HD, :] = (g2 * cos_a - g1 * sin_a).astype(BF16)
            dkv_ref[HD:2 * HD, :] = dv[...].T.astype(BF16)


def attn_bwd(scal, qr, d_o, o_t, lse, qkv_t, cos_t, sin_t, qs_row, start, count, carry=None):
    width = count * BQ
    last = carry is not None
    whole = lambda i, s: (0, 0)
    blocked = lambda i, s: (0, i)
    in_specs = [
        pl.BlockSpec((HEADS * HD, BQ), blocked),
        pl.BlockSpec((HEADS * HD, BQ), blocked),
        pl.BlockSpec((HEADS * HD, BQ), blocked),
        pl.BlockSpec((HEADS, BQ), blocked),
        pl.BlockSpec((2 * HD, 2048), lambda i, s: (4, 0)),
        pl.BlockSpec((HALF, 2048), whole),
        pl.BlockSpec((HALF, 2048), whole),
        pl.BlockSpec((1, 2048), whole),
    ]
    scratch = [
        pltpu.VMEM((2048, HD), BF16),
        pltpu.VMEM((HD, 2048), BF16),
        pltpu.VMEM((2048, HD), BF16),
        pltpu.VMEM((HD, HEADS * BQ), BF16),
        pltpu.VMEM((HD, HEADS * BQ), BF16),
        pltpu.VMEM((HEADS, BQ), F32),
        pltpu.VMEM((HD, HEADS * BQ), F32),
        pltpu.VMEM((BK, BQ), F32),
        pltpu.VMEM((BK, HEADS * BQ), BF16),
        pltpu.VMEM((BK, HEADS * BQ), BF16),
    ]
    out_specs = [pl.BlockSpec((HEADS * HD, BQ), blocked)]
    out_shape = [jax.ShapeDtypeStruct((HEADS * HD, width), BF16)]
    args = [scal, qr, d_o, o_t, lse, qkv_t, cos_t, sin_t, qs_row]
    if last:
        in_specs += [pl.BlockSpec((2048, HD), whole)] * 2
        args += list(carry)
        out_specs += [pl.BlockSpec((2 * HD, 2048), whole)]
        out_shape += [jax.ShapeDtypeStruct((2 * HD, 2048), BF16)]
        scratch = [pltpu.VMEM((2048, HD), F32)] * 2 + scratch
    else:
        out_specs += [pl.BlockSpec((2048, HD), whole)] * 2
        out_shape += [jax.ShapeDtypeStruct((2048, HD), F32)] * 2
    return pl.pallas_call(
        functools.partial(attn_bwd_kernel, start, last),
        grid_spec=pltpu.PrefetchScalarGridSpec(
            num_scalar_prefetch=1, grid=(count,), in_specs=in_specs, out_specs=out_specs, scratch_shapes=scratch),
        out_shape=out_shape,
        compiler_params=pltpu.CompilerParams(dimension_semantics=("arbitrary",), vmem_limit_bytes=56 << 20),
        cost_estimate=pl.CostEstimate(flops=int(25e9), bytes_accessed=8 << 20, transcendentals=0),
        name="attn_bwd",
    )(*args)


def embed_grad_kernel(order_ref, ids_ref, starts_ref, a_ref, b_ref, c_ref, d_ref, out_ref, rows):
    i = pl.program_id(0)

    @pl.when(i == 0)
    def _():
        for r, ref in enumerate((a_ref, b_ref, c_ref, d_ref)):
            def widen(t, carry, r=r, ref=ref):
                src = pl.multiple_of(t * 16, 16)
                rows[pl.ds(pl.multiple_of(r * 512 + t * 16, 16), 16), :] = ref[pl.ds(src, 16), :].astype(F32)
                return carry
            lax.fori_loop(0, 32, widen, 0)

    out_ref[...] = jnp.zeros_like(out_ref)
    base = i * ROWS_OUT

    def add_row(t, carry):
        dst = ids_ref[t] - base
        out_ref[pl.ds(dst, 1), :] += rows[pl.ds(order_ref[t], 1), :]
        return carry

    lax.fori_loop(starts_ref[i], starts_ref[i + 1], add_row, 0)


def embed_grad(order, ids, starts, shards, vocab_local):
    blocks = vocab_local // ROWS_OUT
    whole = lambda i, o, d, s: (0, 0)
    return pl.pallas_call(
        embed_grad_kernel,
        grid_spec=pltpu.PrefetchScalarGridSpec(
            num_scalar_prefetch=3,
            grid=(blocks,),
            in_specs=[pl.BlockSpec((512, 2048), whole)] * 4,
            out_specs=pl.BlockSpec((ROWS_OUT, 2048), lambda i, o, d, s: (i, 0)),
            scratch_shapes=[pltpu.VMEM((2048, 2048), F32)],
        ),
        out_shape=jax.ShapeDtypeStruct((vocab_local, 2048), F32),
        compiler_params=pltpu.CompilerParams(dimension_semantics=("arbitrary",), vmem_limit_bytes=56 << 20),
        cost_estimate=pl.CostEstimate(flops=int(30e9), bytes_accessed=75 << 20, transcendentals=0),
        name="embed_grad",
    )(order, ids, starts, *shards)


def solution(mesh):
    def exch(value, bits):
        return lax.ppermute(value, "tp", [(i, i ^ bits) for i in range(4)])

    def gather_shards(value):
        near = exch(value, 1)
        far = exch(value, 2)
        return value, near, far, exch(far, 1)

    def add_f32(*terms):
        total = terms[0].astype(F32)
        for term in terms[1:]:
            total = total + term.astype(F32)
        return total

    def reduce_shards(own, near, far, diag, gate=None):
        far_sum = add_f32(far, exch(diag, 1)).astype(BF16)
        if gate is not None:
            far_sum, _ = lax.optimization_barrier((far_sum, gate))
        return add_f32(own, exch(near, 1), exch(far_sum, 2))

    def all_sum(value):
        value = value + exch(value, 1)
        return value + exch(value, 2)

    def device_step(tokens, doc_ids, embedding, attn_norm, w_q, w_k, w_v, w_o, mlp_norm, w_gate, w_up, w_down, d_out):
        vocab_local, dim = embedding.shape
        me = lax.axis_index("tp")
        tok_abs = tokens.reshape(4, 512)
        local = [tok_abs[me ^ r] - me * vocab_local for r in range(4)]

        def rows_of(r):
            ids = local[r]
            found = jnp.take(embedding, jnp.clip(ids, 0, vocab_local - 1), axis=0)
            return jnp.where(((ids >= 0) & (ids < vocab_local))[:, None], found, jnp.zeros((), BF16))

        part3 = rows_of(3)
        part2 = rows_of(2)
        part1 = rows_of(1)
        part0 = rows_of(0)
        x_emb = reduce_shards(part0, part1, part2, part3).astype(BF16)

        w_qkv = jnp.concatenate([w_q.reshape(dim, HEADS * HD), w_k.reshape(dim, HD), w_v.reshape(dim, HD)], axis=1)
        w_out = w_o.reshape(HEADS * HD, dim)
        positions = jnp.concatenate([(me ^ r) * 512 + jnp.arange(512) for r in range(4)])
        cos_t, sin_t = rope_tables_t(positions)
        docs = doc_ids.reshape(-1)
        doc_start = jnp.sum((docs[:, None] < docs[None, :]).astype(jnp.int32), axis=0)
        start4 = doc_start.reshape(4, 512)
        qs_row = jnp.concatenate([start4[me ^ r] for r in range(4)]).reshape(1, 2048)
        scal = jnp.concatenate([doc_start[::BQ] // BK, me.reshape(1).astype(jnp.int32)])

        keys = jnp.concatenate(local)
        keys = jnp.where((keys >= 0) & (keys < vocab_local), keys, vocab_local)
        sorted_ids, order = lax.sort((keys, jnp.arange(2048, dtype=jnp.int32)), num_keys=1)
        edges = jnp.arange(0, vocab_local + 1, ROWS_OUT, dtype=jnp.int32)
        starts = jnp.sum((sorted_ids[None, :] < edges[:, None]).astype(jnp.int32), axis=1)

        h_one, inv_one = rms_forward(x_emb, attn_norm)
        h_sh = gather_shards(h_one)
        h_near = jnp.concatenate(h_sh[:2])
        h_far = jnp.concatenate(h_sh[2:])
        qkv_t = jnp.concatenate([dot(w_qkv, h_near, 0, 1).astype(BF16), dot(w_qkv, h_far, 0, 1).astype(BF16)], axis=1)

        d_out_late, _ = lax.optimization_barrier((d_out.reshape(512, dim), h_sh[2]))
        do_sh = gather_shards(d_out_late)
        do_near = jnp.concatenate(do_sh[:2])
        do_far = jnp.concatenate(do_sh[2:])

        o_far, qr_far, lse_far = attn_fwd(scal, qkv_t, cos_t, sin_t, qs_row, 4, 4)
        ap_far = dot(o_far, w_out, 0, 0).astype(BF16)
        o_near, qr_near, lse_near = attn_fwd(scal, qkv_t, cos_t, sin_t, qs_row, 0, 4)
        ap_near = dot(o_near, w_out, 0, 0).astype(BF16)
        attn_sum = reduce_shards(ap_near[:512], ap_near[512:], ap_far[:512], ap_far[512:]).astype(BF16)
        x_mid = (x_emb.astype(F32) + attn_sum.astype(F32)).astype(BF16)

        h_two, inv_two = rms_forward(x_mid, mlp_norm)
        h2_sh = gather_shards(h_two)

        def mlp(h_half, do_half):
            gate = dot(h_half, w_gate, 1, 0).astype(BF16)
            up = dot(h_half, w_up, 1, 0).astype(BF16)
            gate32 = gate.astype(F32)
            up32 = up.astype(F32)
            sig = jax.nn.sigmoid(gate32)
            act = gate32 * sig
            mid = (act * up32).astype(BF16)
            d_mid = dot(do_half, w_down, 1, 1)
            d_up = (d_mid * act).astype(BF16)
            d_gate = (d_mid * up32 * sig * (1.0 + gate32 * (1.0 - sig))).astype(BF16)
            d_h = (dot(d_gate, w_gate, 1, 1) + dot(d_up, w_up, 1, 1)).astype(BF16)
            return mid, d_up, d_gate, d_h

        h2_near = jnp.concatenate(h2_sh[:2])
        h2_far = jnp.concatenate(h2_sh[2:])
        mid_near, du_near, dg_near, dh2_near = mlp(h2_near, do_near)
        mid_far, du_far, dg_far, dh2_far = mlp(h2_far, do_far)
        d_h_two = reduce_shards(dh2_near[:512], dh2_near[512:], dh2_far[:512], dh2_far[512:])

        d_mid_norm, d_mlp_norm = rms_backward(d_h_two, x_mid, inv_two, mlp_norm)
        d_x_mid32 = d_out.reshape(512, dim).astype(F32) + d_mid_norm
        dx_sh = gather_shards(d_x_mid32.astype(BF16))
        dx_near = jnp.concatenate(dx_sh[:2])
        dx_far = jnp.concatenate(dx_sh[2:])

        down_near = dot(mid_near, w_down, 1, 0).astype(BF16)
        down_far = dot(mid_far, w_down, 1, 0).astype(BF16)
        y_sum = reduce_shards(down_near[:512], down_near[512:], down_far[:512], down_far[512:], gate=dx_sh[2])
        y_out = (x_mid.astype(F32) + y_sum.astype(BF16).astype(F32)).astype(BF16).reshape(1, 512, dim)

        da_near = dot(w_out, dx_near, 1, 1).astype(BF16)
        da_far = dot(w_out, dx_far, 1, 1).astype(BF16)
        dq_near, dk_acc, dv_acc = attn_bwd(scal, qr_near, da_near, o_near, lse_near, qkv_t, cos_t, sin_t, qs_row, 0, 4)
        dq_far, dkv_t = attn_bwd(scal, qr_far, da_far, o_far, lse_far, qkv_t, cos_t, sin_t, qs_row, 4, 4,
                                 carry=(dk_acc, dv_acc))
        dqkv_far = jnp.concatenate([dq_far, dkv_t[:, 1024:]], axis=0)
        dqkv_near = jnp.concatenate([dq_near, dkv_t[:, :1024]], axis=0)
        dh1_far = dot(dqkv_far, w_qkv, 0, 1).astype(BF16)
        dh1_near = dot(dqkv_near, w_qkv, 0, 1).astype(BF16)
        d_h_one = reduce_shards(dh1_near[:512], dh1_near[512:], dh1_far[:512], dh1_far[512:])

        d_emb_norm, d_attn_norm = rms_backward(d_h_one, x_emb, inv_one, attn_norm)
        dxe_sh = gather_shards((d_x_mid32 + d_emb_norm).astype(BF16))
        d_embedding = embed_grad(order, sorted_ids, starts, dxe_sh, vocab_local)

        mid_all = jnp.concatenate([mid_near, mid_far])
        do_all = jnp.concatenate([do_near, do_far])
        h2_all = jnp.concatenate([h2_near, h2_far])
        d_w_down = dot(mid_all, do_all, 0, 0)
        d_w_gate = dot(h2_all, jnp.concatenate([dg_near, dg_far]), 0, 0)
        d_w_up = dot(h2_all, jnp.concatenate([du_near, du_far]), 0, 0)
        d_w_o = dot(jnp.concatenate([o_near, o_far], axis=1), jnp.concatenate([dx_near, dx_far]), 1, 0)
        d_w_qkv = dot(jnp.concatenate([h_near, h_far]), jnp.concatenate([dqkv_near, dqkv_far], axis=1), 0, 1)
        d_w_q = d_w_qkv[:, :HEADS * HD].reshape(dim, HEADS, HD)
        d_w_k = d_w_qkv[:, HEADS * HD:HEADS * HD + HD].reshape(dim, 1, HD)
        d_w_v = d_w_qkv[:, HEADS * HD + HD:].reshape(dim, 1, HD)
        gains = all_sum(jnp.stack([d_attn_norm, d_mlp_norm]))
        return (y_out, d_embedding, gains[0], d_w_q, d_w_k, d_w_v, d_w_o.reshape(HEADS, HD, dim), gains[1],
                d_w_gate, d_w_up, d_w_down)

    in_specs = (P("dp", None), P("dp", None), P("tp", None), P(None), P(None, "tp", None), P(None, "tp", None),
                P(None, "tp", None), P("tp", None, None), P(None), P(None, "tp"), P(None, "tp"), P("tp", None),
                P("dp", "tp", None))
    out_specs = (P("dp", "tp", None), P(("dp", "tp"), None), P("dp"), P("dp", "tp", None), P("dp", "tp", None),
                 P("dp", "tp", None), P(("dp", "tp"), None, None), P("dp"), P("dp", "tp"), P("dp", "tp"),
                 P(("dp", "tp"), None))
    return jax.shard_map(device_step, mesh=mesh, in_specs=in_specs, out_specs=out_specs, check_vma=False)
```

time: 1450 us -> 914 us (0.63)
  matrix products: 583 us -> 239 us
  other arithmetic: 309 us -> 62 us
  Pallas kernels: 0 us -> 164 us
  waiting for transfers between devices: 452 us -> 333 us
  starting transfers between devices: 0.62 us -> 47 us
    dot_general x25, matrix products: 572 us -> 239 us  [dot(): lax.dot_general(a, b, (((ca,), (cb,)), ((), ())), preferred_element_type=...]
    ppermute x0 -> x32, waiting for transfers between devices: none -> 333 us  [exch(): return lax.ppermute(value, 'tp', [(i, i ^ bits) for i in range(4)])]
    reduce_scatter x5 -> x0, waiting for transfers between devices: 266 us -> none  [the longest x1 101 us: device_step(): x_emb = lax.psum_scatter(x_part, 'tp', scatter_dimension=1, tiled=True)]
    all_gather x5 -> x0, waiting for transfers between devices: 185 us -> none  [the longest x1 55.8 us: device_step(): d_x_mid_full = lax.all_gather(d_x_mid, 'tp', axis=1, tiled=True)]
    pallas_call x0 -> x5, Pallas kernels: none -> 164 us  [the longest x2 69.5 us: attn_fwd(): pl.pallas_call(functools.partial(attn_fwd_kernel, start), grid_spec=pltpu...]
    another operation x1, other arithmetic: 106 us -> 0.02 us  [device_step(): gains = all_sum(jnp.stack([d_attn_norm, d_mlp_norm]))]
    scatter-add x3 -> x0, other arithmetic: 92.2 us -> none  [device_step(): jax.ops.segment_sum(d_x_full.reshape(-1, model_dim).astype(jnp.float32),...]
    ppermute x0 -> x32, starting transfers between devices: none -> 47 us  [exch(): return lax.ppermute(value, 'tp', [(i, i ^ bits) for i in range(4)])]
  transfers between devices with their start and end apart: 10 -> 32, of which waited for: 9 -> 10; matrix products, arithmetic and copies ran while one was open for 13% -> 32% of each run, Pallas kernels for 0% -> 8%
where the time goes in v1:
time: 914 us; the launch traced here: 920 us
  waiting for transfers between devices  333 us (36%)
  matrix products  239 us (26%)
  Pallas kernels  164 us (18%)
  local copies, waits for them, and re-layouts  73.7 us (8%)
  other arithmetic  62 us (7%)
  starting transfers between devices  47 us (5%)
    ppermute x32, waiting for transfers between devices, exch(): return lax.ppermute(value, 'tp', [(i, i ^ bits) for i in range(4)])  333 us
    dot_general x25, matrix products, dot(): lax.dot_general(a, b, (((ca,), (cb,)), ((), ())), preferred_element_type=...  239 us
    pallas_call x2, Pallas kernels, attn_fwd(): pl.pallas_call(functools.partial(attn_fwd_kernel, start), grid_spec=pltpu...  69.5 us
    pallas_call x2, Pallas kernels, attn_bwd(): pl.pallas_call(functools.partial(attn_bwd_kernel, start, last), grid_spec...  52.4 us
    gather x4, local copies, waits for them, and re-layouts, rows_of(): found = jnp.take(embedding, jnp.clip(ids, 0, vocab_local - 1), axis=0)  47.1 us
    ppermute x32, starting transfers between devices, exch(): return lax.ppermute(value, 'tp', [(i, i ^ bits) for i in range(4)])  47 us
    pallas_call x1, Pallas kernels, embed_grad(): pl.pallas_call(embed_grad_kernel, grid_spec=pltpu.PrefetchScalarGridSpec(...  42.2 us
  transfers between devices with their start and end apart: 32, of which 10 were waited for; matrix products, arithmetic and copies ran while one was open for 32% of the time, Pallas kernels for 8%

profile of v1, /device:TPU:0, one launch (start us, length us, event | category | flops | bytes accessed | tf_op | source)
XLA Modules:
  0.0 920.2 jit_solution(8758900696217663404)
XLA Ops:
  2.8 11.5 %gather_fusion.3 = bf16[512,2048]{1,0:T(8,128)(2,1)} fusion(bf16[8000,2048]{1,0:T(8,128)(2,1)} %param.17, s32[1024]{0:T(1024)S(1)} %pad_clamp_fusion), kind=kCustom, calls=%fused_computation.3.clone | custom fusion | bytes 4196352 | tf_op jit(solution)/shard_map/jit(_take)/gather | solution.py:358
  22.7 11.8 %gather_fusion.1 = bf16[512,2048]{1,0:T(8,128)(2,1)} fusion(bf16[8000,2048]{1,0:T(8,128)(2,1)} %param.17, s32[1024]{0:T(1024)S(1)} %pad_clamp_fusion.2), kind=kCustom, calls=%fused_computation.1.clone | custom fusion | bytes 4196352 | tf_op jit(solution)/shard_map/jit(_take)/gather | solution.py:358
  41.2 11.4 %gather_fusion.2 = bf16[512,2048]{1,0:T(8,128)(2,1)} fusion(bf16[8000,2048]{1,0:T(8,128)(2,1)} %param.17, s32[1024]{0:T(1024)S(1)} %pad_clamp_fusion.1), kind=kCustom, calls=%fused_computation.2.clone | custom fusion | bytes 4196352 | tf_op jit(solution)/shard_map/jit(_take)/gather | solution.py:358
  57.0 17.6 %collective-permute-start.2 = (bf16[512,2048]{1,0:T(8,128)(2,1)}, bf16[512,2048]{1,0:T(8,128)(2,1)}, u32[]{:S(2)}, u32[]{:S(2)}) collective-permute-start(bf16[512,2048]{1,0:T(8,128)(2,1)} %add_convert_fusion.9), channel_id=1, source_target_pairs={{0,2},{1,3},{2,0},{3,1},{4,6},{5,7},{6,4},{7,5}} | collective-permute-start | bytes 6291464 | tf_op jit(solution)/shard_map/ppermute | solution.py:327
  74.6 12.4 %gather_fusion = bf16[512,2048]{1,0:T(8,128)(2,1)} fusion(bf16[8000,2048]{1,0:T(8,128)(2,1)} %param.17, s32[1024]{0:T(1024)S(1)} %pad_clamp_fusion.3), kind=kCustom, calls=%fused_computation.clone | custom fusion | bytes 4196352 | tf_op jit(solution)/shard_map/jit(_take)/gather | solution.py:358
  87.1 32.1 %collective-permute-done.2 = bf16[512,2048]{1,0:T(8,128)(2,1)} collective-permute-done((bf16[512,2048]{1,0:T(8,128)(2,1)}, bf16[512,2048]{1,0:T(8,128)(2,1)}, u32[]{:S(2)}, u32[]{:S(2)}) %collective-permute-start.2) | collective-permute-done | bytes 2097184 | tf_op jit(solution)/shard_map/ppermute | solution.py:327
  129.6 44.6 %collective-permute-done.4 = bf16[512,2048]{1,0:T(8,128)(2,1)} collective-permute-done((bf16[512,2048]{1,0:T(8,128)(2,1)}, bf16[512,2048]{1,0:T(8,128)(2,1)}, u32[]{:S(2)}, u32[]{:S(2)}) %collective-permute-start.4) | collective-permute-done | bytes 2097184 | tf_op jit(solution)/shard_map/ppermute | solution.py:327
  189.2 45.8 %attn_fwd.3 = (bf16[512,1024]{1,0:T(8,128)(2,1)S(1)}, bf16[512,1024]{1,0:T(8,128)(2,1)S(1)}, f32[8,1024]{1,0:T(8,128)S(1)}) custom-call(s32[9]{0:T(128)S(1)} %pad_add_fusion.2.s_ref, bf16[640,2048]{1,0:T(8,128)(2,1)S(1)} %pad_maximum_fusion.5.q_ref.kv_ref, bf16[640,2048]{1,0:T(8,128)(2,1)S(1)} %pad_maximum_fusion.5.q_ref.kv_ref, ...), custom_call_target="tpu_custom_call" | custom-call | flops 10000000000 | bytes 8388608 | tf_op jit(solution)/shard_map/attn_fwd/pallas_call | solution.py:123
  237.8 23.7 %attn_fwd.2 = (bf16[512,1024]{1,0:T(8,128)(2,1)S(1)}, bf16[512,1024]{1,0:T(8,128)(2,1)S(1)}, f32[8,1024]{1,0:T(8,128)S(1)}) custom-call(s32[9]{0:T(128)S(1)} %pad_add_fusion.2.s_ref, bf16[640,2048]{1,0:T(8,128)(2,1)S(1)} %pad_maximum_fusion.5.q_ref.kv_ref, bf16[640,2048]{1,0:T(8,128)(2,1)S(1)} %pad_maximum_fusion.5.q_ref.kv_ref, ...), custom_call_target="tpu_custom_call" | custom-call | flops 10000000000 | bytes 8388608 | tf_op jit(solution)/shard_map/attn_fwd/pallas_call | solution.py:123
  268.5 45.6 %collective-permute-done.8 = bf16[512,2048]{1,0:T(8,128)(2,1)S(1)} collective-permute-done((bf16[512,2048]{1,0:T(8,128)(2,1)S(1)}, bf16[512,2048]{1,0:T(8,128)(2,1)S(1)}, u32[]{:S(2)}, u32[]{:S(2)}) %collective-permute-start.8) | collective-permute-done | bytes 2097184 | tf_op jit(solution)/shard_map/ppermute | solution.py:327
  327.3 31.7 %collective-permute-done.16 = bf16[512,2048]{1,0:T(8,128)(2,1)} collective-permute-done((bf16[512,2048]{1,0:T(8,128)(2,1)}, bf16[512,2048]{1,0:T(8,128)(2,1)}, u32[]{:S(2)}, u32[]{:S(2)}) %collective-permute-start.16) | collective-permute-done | bytes 2097184 | tf_op jit(solution)/shard_map/ppermute | solution.py:327
  359.1 44.5 %collective-permute-done.11 = bf16[512,2048]{1,0:T(8,128)(2,1)} collective-permute-done((bf16[512,2048]{1,0:T(8,128)(2,1)}, bf16[512,2048]{1,0:T(8,128)(2,1)}, u32[]{:S(2)}, u32[]{:S(2)}) %collective-permute-start.11) | collective-permute-done | bytes 2097184 | tf_op jit(solution)/shard_map/ppermute | solution.py:327
  403.5 11.3 %convolution_convert_fusion.2 = bf16[1024,1408]{1,0:T(8,128)(2,1)} fusion(bf16[2048,1408]{1,0:T(8,128)(2,1)} %param.25, bf16[512,2048]{1,0:T(8,128)(2,1)} %collective-permute-done.9, bf16[512,2048]{1,0:T(8,128)(2,1)} %fusion.68), kind=kOutput, calls=%fused_computation.139 | convolution fusion | flops 5915410432 | bytes 12845056 | tf_op jit(solution)/shard_map/dot_general | solution.py:36
  414.9 10.2 %convolution_convert_fusion.3 = bf16[1024,1408]{1,0:T(8,128)(2,1)} fusion(bf16[2048,1408]{1,0:T(8,128)(2,1)S(1)} %bitcast.94, bf16[512,2048]{1,0:T(8,128)(2,1)} %collective-permute-done.9, bf16[512,2048]{1,0:T(8,128)(2,1)} %fusion.68), kind=kOutput, calls=%fused_computation.140 | convolution fusion | flops 5915410432 | bytes 12845056 | tf_op jit(solution)/shard_map/dot_general | solution.py:36
  425.1 15.4 %multiply_convert_fusion.1 = (bf16[1024,1408]{1,0:T(8,128)(2,1)}, bf16[1024,1408]{1,0:T(8,128)(2,1)}, bf16[1024,1408]{1,0:T(8,128)(2,1)}) fusion(bf16[1024,1408]{1,0:T(8,128)(2,1)} %convolution_convert_fusion.3, bf16[1024,1408]{1,0:T(8,128)(2,1)} %convolution_convert_fusion.2, bf16[1408,2048]{1,0:T(8,128)(2,1)} %param.26, ...), kind=kOutput, calls=%fused_computation.84 | convolution fusion | flops 5938479104 | bytes 24379392 | tf_op jit(solution)/shard_map/dot_general | solution.py:36
  443.0 8.9 fusion.156
  452.1 11.1 %convolution_convert_fusion = bf16[1024,1408]{1,0:T(8,128)(2,1)} fusion(bf16[1024,2048]{1,0:T(8,128)(2,1)S(1)} %constant_dynamic-update-slice_fusion, bf16[2048,1408]{1,0:T(8,128)(2,1)} %param.25), kind=kOutput, calls=%fused_computation.137 | convolution fusion | flops 5907021824 | bytes 12845056 | tf_op jit(solution)/shard_map/dot_general | solution.py:36
  471.2 15.5 %multiply_convert_fusion = (bf16[1024,1408]{1,0:T(8,128)(2,1)}, bf16[1024,1408]{1,0:T(8,128)(2,1)}, bf16[1024,1408]{1,0:T(8,128)(2,1)}) fusion(bf16[1024,1408]{1,0:T(8,128)(2,1)} %convolution_convert_fusion.1, bf16[1024,1408]{1,0:T(8,128)(2,1)} %convolution_convert_fusion, bf16[1408,2048]{1,0:T(8,128)(2,1)} %param.26, ...), kind=kOutput, calls=%fused_computation.83 | convolution fusion | flops 5938479104 | bytes 24379392 | tf_op jit(solution)/shard_map/dot_general | solution.py:36
  486.6 10.5 %fusion.157 = f32[1024,2048]{1,0:T(8,128)} fusion(bf16[1024,1408]{1,0:T(8,128)(2,1)} %get-tuple-element.55, bf16[2048,1408]{1,0:T(8,128)(2,1)S(1)} %bitcast.94), kind=kOutput, calls=%fused_computation.248 | convolution fusion | flops 5905580032 | bytes 17039360 | tf_op jit(solution)/shard_map/dot_general | solution.py:36
  497.1 11.0 %add_convert_fusion = bf16[1024,2048]{1,0:T(8,128)(2,1)S(1)} fusion(f32[1024,2048]{1,0:T(8,128)} %fusion.157, bf16[1024,1408]{1,0:T(8,128)(2,1)S(1)} %copy-done.58, bf16[2048,1408]{1,0:T(8,128)(2,1)} %param.25), kind=kOutput, calls=%fused_computation.36 | convolution fusion | flops 5909774336 | bytes 21233664 | tf_op jit(solution)/shard_map/dot_general | solution.py:36
  508.9 10.9 %add_convert_fusion.1 = bf16[1024,2048]{1,0:T(8,128)(2,1)S(1)} fusion(f32[1024,2048]{1,0:T(8,128)} %fusion.156, bf16[1024,1408]{1,0:T(8,128)(2,1)} %get-tuple-element.52, bf16[2048,1408]{1,0:T(8,128)(2,1)} %param.25), kind=kOutput, calls=%fused_computation.37 | convolution fusion | flops 5909774336 | bytes 21233664 | tf_op jit(solution)/shard_map/dot_general | solution.py:36
  542.3 26.8 %collective-permute-done.19 = bf16[512,2048]{1,0:T(8,128)(2,1)S(1)} collective-permute-done((bf16[512,2048]{1,0:T(8,128)(2,1)S(1)}, bf16[512,2048]{1,0:T(8,128)(2,1)S(1)}, u32[]{:S(2)}, u32[]{:S(2)}) %collective-permute-start.19) | collective-permute-done | bytes 2097184 | tf_op jit(solution)/shard_map/ppermute | solution.py:327
  578.8 19.1 %fusion.16 = f32[1408,2048]{1,0:T(8,128)} fusion(bf16[512,2048]{1,0:T(8,128)(2,1)} %collective-permute-done.17, bf16[512,2048]{1,0:T(8,128)(2,1)} %collective-permute-done.16, bf16[512,2048]{1,0:T(8,128)(2,1)} %collective-permute-done.14, bf16[512,2048]{1,0:T(8,128)(2,1)} %bitcast.15, bf16[1024,1408]{1,0:T(8,128)(2,1)} %get-tuple-element.56, ...), kind=kOutput, calls=%fused_computation.28 | convolution fusion | flops 11856248832 | bytes 25690112 | tf_op jit(solution)/shard_map/dot_general | solution.py:36
  602.8 22.3 %collective-permute-done.20 = bf16[512,2048]{1,0:T(8,128)(2,1)} collective-permute-done((bf16[512,2048]{1,0:T(8,128)(2,1)S(1)}, bf16[512,2048]{1,0:T(8,128)(2,1)}, u32[]{:S(2)}, u32[]{:S(2)}) %collective-permute-start.20) | collective-permute-done | bytes 2097184 | tf_op jit(solution)/shard_map/ppermute | solution.py:327
  625.1 18.7 %attn_bwd.2 = (bf16[512,1024]{1,0:T(8,128)(2,1)}, f32[2048,64]{1,0:T(8,128)}, f32[2048,64]{1,0:T(8,128)}) custom-call(s32[9]{0:T(128)} %copy-done.5, bf16[512,1024]{1,0:T(8,128)(2,1)} %copy-done.11, bf16[512,1024]{1,0:T(8,128)(2,1)} %fusion.123.do_ref, bf16[512,1024]{1,0:T(8,128)(2,1)} %copy-done.8, f32[8,1024]{1,0:T(8,128)} %copy-done.13, ...), custom_call_target="tpu_custom_call" | custom-call | flops 24999999488 | bytes 8388608 | tf_op jit(solution)/shard_map/attn_bwd/pallas_call | solution.py:272
  649.5 33.7 %attn_bwd.3 = (bf16[512,1024]{1,0:T(8,128)(2,1)}, bf16[128,2048]{1,0:T(8,128)(2,1)}) custom-call(s32[9]{0:T(128)} %copy-done.5, bf16[512,1024]{1,0:T(8,128)(2,1)} %copy-done.10, bf16[512,1024]{1,0:T(8,128)(2,1)} %fusion.126.do_ref, bf16[512,1024]{1,0:T(8,128)(2,1)} %copy-done.6, f32[8,1024]{1,0:T(8,128)} %copy-done.12, bf16[640,2048]{1,0:T(8,128)(2,1)} %copy-done.1, ...), custom_call_target="tpu_custom_call" | custom-call | flops 24999999488 | bytes 8388608 | tf_op jit(solution)/shard_map/attn_bwd/pallas_call | solution.py:272
  693.6 19.9 %fusion.52 = f32[2048,1408]{1,0:T(8,128)} fusion(bf16[1024,1408]{1,0:T(8,128)(2,1)} %get-tuple-element.54, bf16[1024,1408]{1,0:T(8,128)(2,1)} %get-tuple-element.52, bf16[512,2048]{1,0:T(8,128)(2,1)S(1)} %copy-done.31, bf16[512,2048]{1,0:T(8,128)(2,1)} %collective-permute-done.11, bf16[512,2048]{1,0:T(8,128)(2,1)} %collective-permute-done.9, ...), kind=kOutput, calls=%fused_computation.76 | convolution fusion | flops 11856248832 | bytes 25690112 | tf_op jit(solution)/shard_map/dot_general | solution.py:36
  728.9 20.0 %fusion.48 = f32[2048,1408]{1,0:T(8,128)} fusion(bf16[1024,1408]{1,0:T(8,128)(2,1)} %get-tuple-element.55, bf16[1024,1408]{1,0:T(8,128)(2,1)} %get-tuple-element.53, bf16[512,2048]{1,0:T(8,128)(2,1)} %copy-done.30, bf16[512,2048]{1,0:T(8,128)(2,1)} %collective-permute-done.11, bf16[512,2048]{1,0:T(8,128)(2,1)} %collective-permute-done.9, ...), kind=kOutput, calls=%fused_computation.72 | convolution fusion | flops 11856248832 | bytes 25690112 | tf_op jit(solution)/shard_map/dot_general | solution.py:36
  753.9 21.8 %collective-permute-done.26 = bf16[512,2048]{1,0:T(8,128)(2,1)} collective-permute-done((bf16[512,2048]{1,0:T(8,128)(2,1)}, bf16[512,2048]{1,0:T(8,128)(2,1)}, u32[]{:S(2)}, u32[]{:S(2)}) %collective-permute-start.26) | collective-permute-done | bytes 2097184 | tf_op jit(solution)/shard_map/ppermute | solution.py:327
  793.6 8.5 fusion
  802.7 62.4 %collective-permute-done.28.c_ref = bf16[512,2048]{1,0:T(8,128)(2,1)} collective-permute-done((bf16[512,2048]{1,0:T(8,128)(2,1)}, bf16[512,2048]{1,0:T(8,128)(2,1)}, u32[]{:S(2)}, u32[]{:S(2)}) %collective-permute-start.28) | collective-permute-done | bytes 2097184 | tf_op jit(solution)/shard_map/ppermute | solution.py:327
  877.7 42.2 %embed_grad.1 = f32[8000,2048]{1,0:T(8,128)} custom-call(s32[2048]{0:T(1024)} %get-tuple-element.31.order_ref, s32[2048]{0:T(1024)} %copy-done.41, s32[41]{0:T(128)} %convert_reduce_fusion.1.starts_ref, bf16[512,2048]{1,0:T(8,128)(2,1)} %fusion.64.a_ref, bf16[512,2048]{1,0:T(8,128)(2,1)} %copy-done.48, bf16[512,2048]{1,0:T(8,128)(2,1)} %collective-permute-done.28.c_ref, ...), custom_call_target="tpu_custom_call" | custom-call | flops 30000001024 | bytes 78643200 | tf_op jit(solution)/shard_map/embed_grad/pallas_call | solution.py:309
  (264 shorter events, 185.2 us)
Async XLA Ops:
  17.5 35.1 %collective-permute-start.1 = (bf16[512,2048]{1,0:T(8,128)(2,1)}, bf16[512,2048]{1,0:T(8,128)(2,1)}, u32[]{:S(2)}, u32[]{:S(2)}) collective-permute-start(bf16[512,2048]{1,0:T(8,128)(2,1)} %select_select_fusion), channel_id=1, source_target_pairs={{0,1},{1,0},{2,3},{3,2},{4,5},{5,4},{6,7},{7,6}} | collective-permute-start | bytes 6291464 | tf_op jit(solution)/shard_map/ppermute | solution.py:327
  37.7 49.3 %collective-permute-start = (bf16[512,2048]{1,0:T(8,128)(2,1)}, bf16[512,2048]{1,0:T(8,128)(2,1)}, u32[]{:S(2)}, u32[]{:S(2)}) collective-permute-start(bf16[512,2048]{1,0:T(8,128)(2,1)} %select_select_fusion.2), channel_id=1, source_target_pairs={{0,1},{1,0},{2,3},{3,2},{4,5},{5,4},{6,7},{7,6}} | collective-permute-start | bytes 6291464 | tf_op jit(solution)/shard_map/ppermute | solution.py:327
  57.0 62.2 %collective-permute-start.2 = (bf16[512,2048]{1,0:T(8,128)(2,1)}, bf16[512,2048]{1,0:T(8,128)(2,1)}, u32[]{:S(2)}, u32[]{:S(2)}) collective-permute-start(bf16[512,2048]{1,0:T(8,128)(2,1)} %add_convert_fusion.9), channel_id=1, source_target_pairs={{0,2},{1,3},{2,0},{3,1},{4,6},{5,7},{6,4},{7,5}} | collective-permute-start | bytes 6291464 | tf_op jit(solution)/shard_map/ppermute | solution.py:327
  126.2 48.0 %collective-permute-start.4 = (bf16[512,2048]{1,0:T(8,128)(2,1)}, bf16[512,2048]{1,0:T(8,128)(2,1)}, u32[]{:S(2)}, u32[]{:S(2)}) collective-permute-start(bf16[512,2048]{1,0:T(8,128)(2,1)} %fusion.59), channel_id=1, source_target_pairs={{0,2},{1,3},{2,0},{3,1},{4,6},{5,7},{6,4},{7,5}} | collective-permute-start | bytes 6291464 | tf_op jit(solution)/shard_map/ppermute | solution.py:327
  128.5 49.3 %collective-permute-start.3 = (bf16[512,2048]{1,0:T(8,128)(2,1)}, bf16[512,2048]{1,0:T(8,128)(2,1)}, u32[]{:S(2)}, u32[]{:S(2)}) collective-permute-start(bf16[512,2048]{1,0:T(8,128)(2,1)} %fusion.59), channel_id=1, source_target_pairs={{0,1},{1,0},{2,3},{3,2},{4,5},{5,4},{6,7},{7,6}} | collective-permute-start | bytes 6291464 | tf_op jit(solution)/shard_map/ppermute | solution.py:327
  174.2 9.6 %collective-permute-start.5 = (bf16[512,2048]{1,0:T(8,128)(2,1)}, bf16[512,2048]{1,0:T(8,128)(2,1)}, u32[]{:S(2)}, u32[]{:S(2)}) collective-permute-start(bf16[512,2048]{1,0:T(8,128)(2,1)} %collective-permute-done.4), channel_id=1, source_target_pairs={{0,1},{1,0},{2,3},{3,2},{4,5},{5,4},{6,7},{7,6}} | collective-permute-start | bytes 6291464 | tf_op jit(solution)/shard_map/ppermute | solution.py:327
  237.7 27.0 %collective-permute-start.7 = (bf16[512,2048]{1,0:T(8,128)(2,1)S(1)}, bf16[512,2048]{1,0:T(8,128)(2,1)S(1)}, u32[]{:S(2)}, u32[]{:S(2)}) collective-permute-start(bf16[512,2048]{1,0:T(8,128)(2,1)S(1)} %slice.107), channel_id=1, source_target_pairs={{0,1},{1,0},{2,3},{3,2},{4,5},{5,4},{6,7},{7,6}} | collective-permute-start | bytes 6291464 | tf_op jit(solution)/shard_map/ppermute | solution.py:327
  264.3 4.3 collective-permute-start.6
  265.6 48.5 %collective-permute-start.8 = (bf16[512,2048]{1,0:T(8,128)(2,1)S(1)}, bf16[512,2048]{1,0:T(8,128)(2,1)S(1)}, u32[]{:S(2)}, u32[]{:S(2)}) collective-permute-start(bf16[512,2048]{1,0:T(8,128)(2,1)S(1)} %add_convert_fusion.7), channel_id=1, source_target_pairs={{0,2},{1,3},{2,0},{3,1},{4,6},{5,7},{6,4},{7,5}} | collective-permute-start | bytes 6291464 | tf_op jit(solution)/shard_map/ppermute | solution.py:327
  267.6 91.4 %collective-permute-start.16 = (bf16[512,2048]{1,0:T(8,128)(2,1)}, bf16[512,2048]{1,0:T(8,128)(2,1)}, u32[]{:S(2)}, u32[]{:S(2)}) collective-permute-start(bf16[512,2048]{1,0:T(8,128)(2,1)} %bitcast.15), channel_id=1, source_target_pairs={{0,2},{1,3},{2,0},{3,1},{4,6},{5,7},{6,4},{7,5}} | collective-permute-start | bytes 6291464 | tf_op jit(solution)/shard_map/ppermute | solution.py:327
  318.9 84.6 %collective-permute-start.11 = (bf16[512,2048]{1,0:T(8,128)(2,1)}, bf16[512,2048]{1,0:T(8,128)(2,1)}, u32[]{:S(2)}, u32[]{:S(2)}) collective-permute-start(bf16[512,2048]{1,0:T(8,128)(2,1)} %fusion.68), channel_id=1, source_target_pairs={{0,2},{1,3},{2,0},{3,1},{4,6},{5,7},{6,4},{7,5}} | collective-permute-start | bytes 6291464 | tf_op jit(solution)/shard_map/ppermute | solution.py:327
  320.9 82.6 %collective-permute-start.9 = (bf16[512,2048]{1,0:T(8,128)(2,1)}, bf16[512,2048]{1,0:T(8,128)(2,1)}, u32[]{:S(2)}, u32[]{:S(2)}) collective-permute-start(bf16[512,2048]{1,0:T(8,128)(2,1)} %fusion.68), channel_id=1, source_target_pairs={{0,1},{1,0},{2,3},{3,2},{4,5},{5,4},{6,7},{7,6}} | collective-permute-start | bytes 6291464 | tf_op jit(solution)/shard_map/ppermute | solution.py:327
  326.8 98.3 %collective-permute-start.14 = (bf16[512,2048]{1,0:T(8,128)(2,1)}, bf16[512,2048]{1,0:T(8,128)(2,1)}, u32[]{:S(2)}, u32[]{:S(2)}) collective-permute-start(bf16[512,2048]{1,0:T(8,128)(2,1)} %bitcast.15), channel_id=1, source_target_pairs={{0,1},{1,0},{2,3},{3,2},{4,5},{5,4},{6,7},{7,6}} | collective-permute-start | bytes 6291464 | tf_op jit(solution)/shard_map/ppermute | solution.py:327
  359.1 112.1 %collective-permute-start.17 = (bf16[512,2048]{1,0:T(8,128)(2,1)}, bf16[512,2048]{1,0:T(8,128)(2,1)}, u32[]{:S(2)}, u32[]{:S(2)}) collective-permute-start(bf16[512,2048]{1,0:T(8,128)(2,1)} %collective-permute-done.16), channel_id=1, source_target_pairs={{0,1},{1,0},{2,3},{3,2},{4,5},{5,4},{6,7},{7,6}} | collective-permute-start | bytes 6291464 | tf_op jit(solution)/shard_map/ppermute | solution.py:327
  403.5 48.3 %collective-permute-start.12 = (bf16[512,2048]{1,0:T(8,128)(2,1)}, bf16[512,2048]{1,0:T(8,128)(2,1)S(1)}, u32[]{:S(2)}, u32[]{:S(2)}) collective-permute-start(bf16[512,2048]{1,0:T(8,128)(2,1)} %collective-permute-done.11), channel_id=1, source_target_pairs={{0,1},{1,0},{2,3},{3,2},{4,5},{5,4},{6,7},{7,6}} | collective-permute-start | bytes 6291464 | tf_op jit(solution)/shard_map/ppermute | solution.py:327
  508.4 11.8 %collective-permute-start.18 = (bf16[512,2048]{1,0:T(8,128)(2,1)S(1)}, bf16[512,2048]{1,0:T(8,128)(2,1)S(1)}, u32[]{:S(2)}, u32[]{:S(2)}) collective-permute-start(bf16[512,2048]{1,0:T(8,128)(2,1)S(1)} %slice.115), channel_id=1, source_target_pairs={{0,1},{1,0},{2,3},{3,2},{4,5},{5,4},{6,7},{7,6}} | collective-permute-start | bytes 6291464 | tf_op jit(solution)/shard_map/ppermute | solution.py:327
  520.1 22.2 %collective-permute-start.15 = (bf16[512,2048]{1,0:T(8,128)(2,1)S(1)}, bf16[512,2048]{1,0:T(8,128)(2,1)S(1)}, u32[]{:S(2)}, u32[]{:S(2)}) collective-permute-start(bf16[512,2048]{1,0:T(8,128)(2,1)S(1)} %slice.113), channel_id=1, source_target_pairs={{0,1},{1,0},{2,3},{3,2},{4,5},{5,4},{6,7},{7,6}} | collective-permute-start | bytes 6291464 | tf_op jit(solution)/shard_map/ppermute | solution.py:327
  521.1 48.0 %collective-permute-start.19 = (bf16[512,2048]{1,0:T(8,128)(2,1)S(1)}, bf16[512,2048]{1,0:T(8,128)(2,1)S(1)}, u32[]{:S(2)}, u32[]{:S(2)}) collective-permute-start(bf16[512,2048]{1,0:T(8,128)(2,1)S(1)} %add_convert_fusion.4), channel_id=1, source_target_pairs={{0,2},{1,3},{2,0},{3,1},{4,6},{5,7},{6,4},{7,5}} | collective-permute-start | bytes 6291464 | tf_op jit(solution)/shard_map/ppermute | solution.py:327
  531.2 333.9 %collective-permute-start.10 = (bf16[512,2048]{1,0:T(8,128)(2,1)}, bf16[512,2048]{1,0:T(8,128)(2,1)}, u32[]{:S(2)}, u32[]{:S(2)}) collective-permute-start(bf16[512,2048]{1,0:T(8,128)(2,1)} %slice.109), channel_id=1, source_target_pairs={{0,1},{1,0},{2,3},{3,2},{4,5},{5,4},{6,7},{7,6}} | collective-permute-start | bytes 6291464 | tf_op jit(solution)/shard_map/ppermute | solution.py:327
  542.1 206.9 %collective-permute-start.13 = (bf16[512,2048]{1,0:T(8,128)(2,1)}, bf16[512,2048]{1,0:T(8,128)(2,1)}, u32[]{:S(2)}, u32[]{:S(2)}) collective-permute-start(bf16[512,2048]{1,0:T(8,128)(2,1)} %slice.111), channel_id=1, source_target_pairs={{0,1},{1,0},{2,3},{3,2},{4,5},{5,4},{6,7},{7,6}} | collective-permute-start | bytes 6291464 | tf_op jit(solution)/shard_map/ppermute | solution.py:327
  577.0 20.8 %collective-permute-start.22 = (bf16[512,2048]{1,0:T(8,128)(2,1)S(1)}, bf16[512,2048]{1,0:T(8,128)(2,1)}, u32[]{:S(2)}, u32[]{:S(2)}) collective-permute-start(bf16[512,2048]{1,0:T(8,128)(2,1)S(1)} %get-tuple-element.46), channel_id=1, source_target_pairs={{0,1},{1,0},{2,3},{3,2},{4,5},{5,4},{6,7},{7,6}} | collective-permute-start | bytes 6291464 | tf_op jit(solution)/shard_map/ppermute | solution.py:327
  577.0 48.0 %collective-permute-start.20 = (bf16[512,2048]{1,0:T(8,128)(2,1)S(1)}, bf16[512,2048]{1,0:T(8,128)(2,1)}, u32[]{:S(2)}, u32[]{:S(2)}) collective-permute-start(bf16[512,2048]{1,0:T(8,128)(2,1)S(1)} %get-tuple-element.46), channel_id=1, source_target_pairs={{0,2},{1,3},{2,0},{3,1},{4,6},{5,7},{6,4},{7,5}} | collective-permute-start | bytes 6291464 | tf_op jit(solution)/shard_map/ppermute | solution.py:327
  625.1 18.7 %collective-permute-start.23 = (bf16[512,2048]{1,0:T(8,128)(2,1)}, bf16[512,2048]{1,0:T(8,128)(2,1)S(1)}, u32[]{:S(2)}, u32[]{:S(2)}) collective-permute-start(bf16[512,2048]{1,0:T(8,128)(2,1)} %collective-permute-done.20), channel_id=1, source_target_pairs={{0,1},{1,0},{2,3},{3,2},{4,5},{5,4},{6,7},{7,6}} | collective-permute-start | bytes 6291464 | tf_op jit(solution)/shard_map/ppermute | solution.py:327
  692.9 28.4 %collective-permute-start.25 = (bf16[512,2048]{1,0:T(8,128)(2,1)}, bf16[512,2048]{1,0:T(8,128)(2,1)}, u32[]{:S(2)}, u32[]{:S(2)}) collective-permute-start(bf16[512,2048]{1,0:T(8,128)(2,1)} %slice.119), channel_id=1, source_target_pairs={{0,1},{1,0},{2,3},{3,2},{4,5},{5,4},{6,7},{7,6}} | collective-permute-start | bytes 6291464 | tf_op jit(solution)/shard_map/ppermute | solution.py:327
  720.7 33.2 %collective-permute-start.24 = (bf16[512,2048]{1,0:T(8,128)(2,1)}, bf16[512,2048]{1,0:T(8,128)(2,1)S(1)}, u32[]{:S(2)}, u32[]{:S(2)}) collective-permute-start(bf16[512,2048]{1,0:T(8,128)(2,1)} %slice.117), channel_id=1, source_target_pairs={{0,1},{1,0},{2,3},{3,2},{4,5},{5,4},{6,7},{7,6}} | collective-permute-start | bytes 6291464 | tf_op jit(solution)/shard_map/ppermute | solution.py:327
  727.2 48.5 %collective-permute-start.26 = (bf16[512,2048]{1,0:T(8,128)(2,1)}, bf16[512,2048]{1,0:T(8,128)(2,1)}, u32[]{:S(2)}, u32[]{:S(2)}) collective-permute-start(bf16[512,2048]{1,0:T(8,128)(2,1)} %add_convert_fusion.2), channel_id=1, source_target_pairs={{0,2},{1,3},{2,0},{3,1},{4,6},{5,7},{6,4},{7,5}} | collective-permute-start | bytes 6291464 | tf_op jit(solution)/shard_map/ppermute | solution.py:327
  753.6 111.5 %collective-permute-start.21 = (bf16[512,2048]{1,0:T(8,128)(2,1)}, bf16[512,2048]{1,0:T(8,128)(2,1)}, u32[]{:S(2)}, u32[]{:S(2)}) collective-permute-start(bf16[512,2048]{1,0:T(8,128)(2,1)} %add_convert_fusion.5), channel_id=1, source_target_pairs={{0,2},{1,3},{2,0},{3,1},{4,6},{5,7},{6,4},{7,5}} | collective-permute-start | bytes 6291464 | tf_op jit(solution)/shard_map/ppermute | solution.py:327
  784.2 80.9 %collective-permute-start.28 = (bf16[512,2048]{1,0:T(8,128)(2,1)}, bf16[512,2048]{1,0:T(8,128)(2,1)}, u32[]{:S(2)}, u32[]{:S(2)}) collective-permute-start(bf16[512,2048]{1,0:T(8,128)(2,1)} %fusion.64.a_ref), channel_id=1, source_target_pairs={{0,2},{1,3},{2,0},{3,1},{4,6},{5,7},{6,4},{7,5}} | collective-permute-start | bytes 6291464 | tf_op jit(solution)/shard_map/ppermute | solution.py:327
  802.1 74.3 %collective-permute-start.27 = (bf16[512,2048]{1,0:T(8,128)(2,1)}, bf16[512,2048]{1,0:T(8,128)(2,1)S(1)}, u32[]{:S(2)}, u32[]{:S(2)}) collective-permute-start(bf16[512,2048]{1,0:T(8,128)(2,1)} %fusion.64.a_ref), channel_id=1, source_target_pairs={{0,1},{1,0},{2,3},{3,2},{4,5},{5,4},{6,7},{7,6}} | collective-permute-start | bytes 6291464 | tf_op jit(solution)/shard_map/ppermute | solution.py:327
  802.2 68.3 %collective-permute-start.30 = (f32[2,2048]{1,0:T(2,128)S(1)}, f32[2,2048]{1,0:T(2,128)S(1)}, u32[]{:S(2)}, u32[]{:S(2)}) collective-permute-start(f32[2,2048]{1,0:T(2,128)S(1)} %pad_maximum_fusion.8), channel_id=1, source_target_pairs={{0,1},{1,0},{2,3},{3,2},{4,5},{5,4},{6,7},{7,6}} | collective-permute-start | bytes 49160 | tf_op jit(solution)/shard_map/ppermute | solution.py:327
  865.1 11.3 %collective-permute-start.29 = (bf16[512,2048]{1,0:T(8,128)(2,1)}, bf16[512,2048]{1,0:T(8,128)(2,1)}, u32[]{:S(2)}, u32[]{:S(2)}) collective-permute-start(bf16[512,2048]{1,0:T(8,128)(2,1)} %collective-permute-done.28.c_ref), channel_id=1, source_target_pairs={{0,1},{1,0},{2,3},{3,2},{4,5},{5,4},{6,7},{7,6}} | collective-permute-start | bytes 6291464 | tf_op jit(solution)/shard_map/ppermute | solution.py:327
  870.5 5.3 collective-permute-start.31
  (63 other events, 1921.3 us)
